TPU v7x, 256 devices: a whole 4x4x8 slice. The times are simulated.
256 devices in a mesh: pop: 64 (over x, z, core), mp: 4 (over y).
Axes of the slice: x: 4, y: 4, z: 8, core: 2. Of those that a mesh axis runs over, the one named last changes fastest.
Arguments:
- tokens: bfloat16 [256, 3584], replicated, may hold values from -60 to 60
- target: bfloat16 [256, 3584], P(None, 'mp'), may hold values from -6 to 6
- w_query: bfloat16 [3584, 3584], P('pop', 'mp'), may hold values from -0.09375 to 0.09375
- w_key: bfloat16 [3584, 512], P(None, 'mp'), may hold values from -0.09375 to 0.09375
- w_value: bfloat16 [3584, 512], P(None, 'mp'), may hold values from -0.09375 to 0.09375
- w_out: bfloat16 [3584, 3584], P('mp', 'pop'), may hold values from -0.09375 to 0.09375
- query_left_factors: bfloat16 [64, 3584, 4], P('pop'), may hold values from -0.09375 to 0.09375
- query_right_factors: bfloat16 [64, 4, 3584], P('pop', None, 'mp'), may hold values from -6 to 6
- o_left: bfloat16 [64, 3584, 4], P('pop', 'mp'), may hold values from -0.09375 to 0.09375
- o_right: bfloat16 [64, 4, 3584], P('pop'), may hold values from -6 to 6
- member_ids: int32 [64], P('pop'), may hold values from 0 to 63, each once
Outputs:
- grad_query: float32 [3584, 3584], P('pop', 'mp')
- grad_out: float32 [3584, 3584], P('mp', 'pop')
- fitness: float32 [64], P('pop')
Inputs may be any that keep to these rules, and one draw needn't show every extreme that they name: `member_ids`: every number from 0 to 63 appears once.
All inputs are finite; a program needn't handle non-finite values.
Results may differ from a plain program's by a relative error of at most 0.005.
Values may be sent and summed in bfloat16 or wider, within the bound.
No kernel may reach another device: no remote copies, remote signals or barrier semaphores. Data moves between devices by JAX's collectives and lax.ppermute only.
A program may use at most 64 MiB of HBM per device.

v0:
```python
import math

import jax
import jax.numpy as jnp
from jax import lax
from jax.sharding import Mesh
from jax.sharding import PartitionSpec as P

D = 3584
HEADS = 28
KV_HEADS = 4
HEAD_DIM = 128
RANK = 4
POP = ("pop_0", "pop_1", "pop_2")


noise_scale = 0.5
rope_base = 1000000.0
spread_floor = 0.001


def in_order(parts, dim):
    parts = jnp.moveaxis(parts, 0, dim)
    shape = parts.shape
    return parts.reshape(*shape[:dim], shape[dim] * shape[dim + 1], *shape[dim + 2 :])


def all_blocks(shard, axes, turns):
    parts = shard[None]
    for k in turns:
        parts = lax.all_gather(parts, axes[k], axis=0, tiled=True)
    held = [lax.axis_size(axes[k]) for k in reversed(turns)]
    parts = parts.reshape(*held, *shard.shape)
    turned = sorted(range(len(turns)), key=lambda place: turns[len(turns) - 1 - place])
    return parts.transpose(*turned, *range(len(turns), parts.ndim)).reshape(-1, *shard.shape)


def whole_of(shard, axes, turns, dim):
    return in_order(all_blocks(shard, axes, turns), dim)


def cut_along(shard, dim, devices):
    before, after = (shard.shape[:dim], shard.shape[dim + 1 :])
    return jnp.moveaxis(shard.reshape(*before, devices, -1, *after), dim, 0)


def summed_on_arrival(shard, axis, dim):
    devices = lax.axis_size(axis)
    parts = lax.all_to_all(cut_along(shard, dim, devices), axis, 0, 0, tiled=True)
    return jnp.sum(parts.astype(jnp.float32), axis=0)


def copy_for_each(shard, axis):
    copies = jnp.broadcast_to(shard, (lax.axis_size(axis), *shard.shape))
    return lax.all_to_all(copies, axis, split_axis=0, concat_axis=0, tiled=True)


def of_everyone(shard, axis):
    return copy_for_each(shard, axis).sum(axis=0)


def gathered_copies(shard, axis, dim):
    return in_order(copy_for_each(shard, axis), dim)


def side_by_side(arrays, axis, dim, along):
    columns = [a.reshape(*a.shape[:along], -1) for a in arrays]
    both = jnp.concatenate(columns, axis=along)
    result, at, done = (lax.all_gather(both, axis, axis=dim, tiled=True), 0, [])
    for a, column in zip(arrays, columns):
        share = result[..., at : at + column.shape[along]]
        done.append(share.reshape(*share.shape[:along], *a.shape[along:]))
        at += column.shape[along]
    return tuple(done)


def tables(count, head_size):
    position = jnp.arange(count, dtype=jnp.float32)
    index = jnp.arange(head_size // 2, dtype=jnp.float32)
    freq = jnp.exp(-math.log(rope_base) * 2.0 * index / head_size)
    angle = position[:, None] * freq[None, :]
    return (jnp.cos(angle)[:, None, :], jnp.sin(angle)[:, None, :])


def rotate(field, cosine_table, sine):
    half = field.shape[-1] // 2
    first = field[..., :half]
    second = field[..., half:]
    return jnp.concatenate(
        [first * cosine_table - second * sine, second * cosine_table + first * sine], axis=-1
    )


def per_device(
    tokens,
    target,
    w_query,
    w_key,
    w_value,
    w_out,
    query_left_factors,
    query_right_factors,
    o_left,
    o_right,
    member_ids,
):
    tok = tokens.shape[0]
    local_feats = w_query.shape[1]
    local_kv = w_key.shape[1] // HEAD_DIM
    group = HEADS // KV_HEADS
    local_heads = local_kv * group
    slots = query_left_factors.shape[0]
    scale = HEAD_DIM ** (-0.5)
    cosine_table, sine = tables(tok, HEAD_DIM)
    base = jnp.dot(tokens, whole_of(w_query, POP, (0, 1, 2), 0), preferred_element_type=jnp.float32)
    keys = rotate(
        jnp.dot(tokens, w_key, preferred_element_type=jnp.float32).reshape(tok, local_kv, HEAD_DIM),
        cosine_table,
        sine,
    ).astype(jnp.bfloat16)
    values = (
        jnp.dot(tokens, w_value, preferred_element_type=jnp.float32)
        .astype(jnp.bfloat16)
        .reshape(tok, local_kv, HEAD_DIM)
    )
    signs = (1 - 2 * (member_ids % 2)).astype(jnp.float32)
    factor = noise_scale * signs[:, None, None]
    lowrank_product = jnp.einsum(
        "td,mdr->mtr", tokens, query_left_factors, preferred_element_type=jnp.float32
    ).astype(jnp.bfloat16)
    query = base[None] + factor * jnp.einsum(
        "olj,ojv->olv", lowrank_product, query_right_factors, preferred_element_type=jnp.float32
    )
    query = rotate(
        query.reshape(slots, tok, local_heads, HEAD_DIM), cosine_table[None], sine[None]
    ).astype(jnp.bfloat16)
    query = query.reshape(slots, tok, local_kv, group, HEAD_DIM)
    scores = jnp.einsum("mtkgd,skd->mkgts", query, keys, preferred_element_type=jnp.float32) * scale
    causal = jnp.arange(tok)[:, None] >= jnp.arange(tok)[None, :]
    scores = jnp.where(causal, scores, -1e30)
    probs = jax.nn.softmax(scores, axis=-1).astype(jnp.bfloat16)
    mixed = (
        jnp.einsum("mkgts,skd->mtkgd", probs, values, preferred_element_type=jnp.float32)
        .astype(jnp.bfloat16)
        .reshape(slots, tok, local_feats)
    )
    low_out = jnp.einsum("mtf,mfr->mtr", mixed, o_left, preferred_element_type=jnp.float32)
    right_full = o_right.astype(jnp.float32)
    part = jnp.einsum(
        "mtf,fe->mte",
        mixed,
        lax.all_gather(w_out, POP, axis=1, tiled=True),
        preferred_element_type=jnp.float32,
    )
    term = part + factor * jnp.einsum(
        "mtr,mre->mte", low_out, right_full, precision=lax.Precision.HIGHEST
    )
    output = summed_on_arrival(term.astype(jnp.bfloat16), "mp", 2)
    diff = output - target.astype(jnp.float32)[None]
    errors = of_everyone(jnp.sum(diff * diff, axis=(1, 2)), "mp")
    fitness = -(errors / (tok * D))
    count = slots * lax.axis_size(POP)
    everyone = gathered_copies(fitness, POP, 0)
    mean = jnp.sum(everyone) / count
    spread = jnp.sum((everyone - mean) * (everyone - mean)) / count
    weight = signs * (fitness - mean) / jnp.sqrt(spread + spread_floor)
    every_weight = gathered_copies(weight, POP, 0)
    right_factors_gathered, left_all = side_by_side((query_right_factors, o_left), POP, 0, 1)
    rows_q = lax.all_to_all(query_left_factors, POP, split_axis=1, concat_axis=0, tiled=True)
    cols_o = lax.all_to_all(o_right, POP, split_axis=2, concat_axis=0, tiled=True)
    whole_population = rows_q.shape[0]
    left_q = jnp.transpose(
        rows_q.astype(jnp.float32) * every_weight[:, None, None], (1, 0, 2)
    ).reshape(rows_q.shape[1], whole_population * RANK)
    right_q = right_factors_gathered.astype(jnp.float32).reshape(
        whole_population * RANK, local_feats
    )
    grad_query = jnp.dot(left_q, right_q, precision=lax.Precision.HIGHEST) / noise_scale
    output_left_factor = jnp.transpose(
        left_all.astype(jnp.float32) * every_weight[:, None, None], (1, 0, 2)
    ).reshape(local_feats, whole_population * RANK)
    right_o = cols_o.astype(jnp.float32).reshape(whole_population * RANK, cols_o.shape[2])
    grad_out = jnp.dot(output_left_factor, right_o, precision=lax.Precision.HIGHEST) / noise_scale
    return (grad_query, grad_out, fitness)


def solution(mesh):
    torus = Mesh(mesh.devices.reshape(4, 8, 2, mesh.shape["mp"]), ("pop_0", "pop_1", "pop_2", "mp"))
    placed = (
        P(),
        P(None, "mp"),
        P(POP, "mp"),
        P(None, "mp"),
        P(None, "mp"),
        P("mp", POP),
        P(POP, None, None),
        P(POP, None, "mp"),
        P(POP, "mp", None),
        P(POP, None, None),
        P(POP),
    )
    return jax.shard_map(
        per_device,
        mesh=torus,
        in_specs=placed,
        out_specs=(P(POP, "mp"), P("mp", POP), P(POP)),
        check_vma=False,
    )
```

profile of v0, /device:TPU:1, one launch (start us, length us, event | category | flops | bytes accessed | tf_op | source)
XLA Modules:
  0.0 428.7 jit_solution(7784847421207332163)
XLA Ops:
  7.2 13.0 %all-gather = bf16[224,896]{1,0:T(8,128)(2,1)} all-gather(bf16[56,896]{1,0:T(8,128)(2,1)} %param.13), channel_id=2, replica_groups=mesh['pop_0'=4,'pop_1'=8,'pop_2'=2,'mp'=4] {'pop_0'}, dimensions={0}, use_global_device_ids=true | all-gather | bytes 501760 | tf_op jit(solution)/shard_map/all_gather | solution.py:31
  20.3 49.6 %all-gather.6.cloned.1.call-done = bf16[32,56,896]{2,1,0:T(8,128)(2,1)} async-done(((bf16[4,56,896]{2,1,0:T(8,128)(2,1)}), bf16[32,56,896]{2,1,0:T(8,128)(2,1)}) %all-gather.6.cloned.1.call-update) | async-done | bytes 3211280 | tf_op jit(solution)/shard_map/all_gather | solution.py:31
  70.0 0.7 all-gather.10.cloned.1.call-update
  71.4 0.7 convolution_bitcast_fusion
  72.2 1.0 fusion.18
  73.6 19.9 %all-gather.8.cloned.1.call-done = bf16[64,56,896]{2,1,0:T(8,128)(2,1)} async-done(((bf16[32,56,896]{2,1,0:T(8,128)(2,1)}), bf16[64,56,896]{2,1,0:T(8,128)(2,1)}) %all-gather.8.cloned.1.call-update) | async-done | bytes 6422544 | tf_op jit(solution)/shard_map/all_gather | solution.py:31
  93.5 3.3 copy.114
  96.9 2.1 fusion.29
  99.1 2.1 fusion.3
  101.1 1.5 copy.115
  102.6 0.9 fusion.27
  103.5 1.3 copy.140
  104.8 1.3 copy.141
  106.1 1.4 fusion.7
  108.2 1.2 copy-done.2
  110.0 2.6 convolution_convert_fusion
  112.8 65.1 %all-gather.10.cloned.1.call-done = bf16[896,3584]{0,1:T(8,128)(2,1)} async-done(((bf16[896,56]{0,1:T(8,128)(2,1)}), bf16[896,3584]{0,1:T(8,128)(2,1)}) %all-gather.10.cloned.1.call-update) | async-done | bytes 6422544 | tf_op jit(solution)/shard_map/all_gather | solution.py:152
  177.9 4.9 %fusion.30 = f32[256,3584]{1,0:T(8,128)S(1)} fusion(bf16[256,896]{0,1:T(8,128)(2,1)S(1)} %bitcast.106, bf16[896,3584]{0,1:T(8,128)(2,1)} %all-gather.10.cloned.1.call-done), kind=kOutput, calls=%fused_computation.58 | convolution fusion | flops 1644167168 | bytes 10551296 | tf_op jit(solution)/shard_map/mtf,fe->mte/dot_general | solution.py:149
  182.8 3.1 fusion.1
  185.9 3.3 reshape.288
  189.2 1.5 copy.145
  190.7 4.0 all-to-all-start.1
  195.3 22.5 %all-to-all-done.1 = bf16[4,1,256,896]{3,2,1,0:T(8,128)(2,1)S(1)} async-done(((bf16[4,1,256,896]{3,2,1,0:T(8,128)(2,1)}), bf16[4,1,256,896]{3,2,1,0:T(8,128)(2,1)S(1)}, u32[]{:S(2)}, u32[]{:S(2)}) %all-to-all-start.1) | async-done | bytes 1835040 | tf_op jit(solution)/shard_map/all_to_all | solution.py:49
  218.1 0.9 multiply_reduce_fusion
  218.9 0.6 broadcast_in_dim.34
  219.6 6.5 %all_to_all.47 = f32[4,1,1]{2,1,0:T(1,128)S(1)} all-to-all(f32[4,1,1]{2,1,0:T(1,128)S(1)} %broadcast_in_dim.34), channel_id=1, replica_groups=mesh['pop_0'=4,'pop_1'=8,'pop_2'=2,'mp'=4] {'mp'}, dimensions={0} | all-to-all | bytes 32 | tf_op jit(solution)/shard_map/all_to_all | solution.py:55
  227.3 0.6 broadcast_in_dim.35
  227.9 7.9 %all-to-all-start.3 = ((f32[64,1,1]{2,1,0:T(1,128)}), f32[64,1,1]{2,1,0:T(1,128)S(1)}, u32[]{:S(2)}, u32[]{:S(2)}) async-start(f32[64,1,1]{2,1,0:T(1,128)} %broadcast_in_dim.35), calls=%async_computation.3 | async-start | bytes 65536 | tf_op jit(solution)/shard_map/all_to_all | solution.py:55
  235.9 51.8 %all-gather.1 = bf16[64,1,7168]{2,1,0:T(2,128)(2,1)S(1)} all-gather(bf16[1,1,7168]{2,1,0:T(2,128)(2,1)S(1)} %maximum_bitcast_fusion.2), channel_id=1, replica_groups=mesh['pop_0'=4,'pop_1'=8,'pop_2'=2,'mp'=4] {'pop_0','pop_1','pop_2'}, dimensions={0}, use_global_device_ids=true | all-gather | bytes 931840 | tf_op jit(solution)/shard_map/all_gather | solution.py:69
  287.7 3.2 copy.129
  290.9 1.2 copy.146
  292.2 7.3 %all-to-all-start.5 = ((bf16[1,4,3584]{1,0,2:T(2,128)(2,1)}), bf16[1,4,3584]{1,0,2:T(2,128)(2,1)S(1)}, u32[]{:S(2)}, u32[]{:S(2)}) async-start(bf16[1,4,3584]{1,0,2:T(2,128)(2,1)} %copy.129), calls=%async_computation.5 | async-start | bytes 3670016 | tf_op jit(solution)/shard_map/all_to_all | solution.py:170
  299.4 2.0 slice_convert_fusion
  301.5 3.2 copy.112
  304.7 0.7 reduce_sum.58
  306.1 38.7 %all-to-all-done.5 = bf16[1,4,3584]{1,0,2:T(2,128)(2,1)S(1)} async-done(((bf16[1,4,3584]{1,0,2:T(2,128)(2,1)}), bf16[1,4,3584]{1,0,2:T(2,128)(2,1)S(1)}, u32[]{:S(2)}, u32[]{:S(2)}) %all-to-all-start.5) | async-done | bytes 28704 | tf_op jit(solution)/shard_map/all_to_all | solution.py:170
  344.8 6.2 %all-to-all-start = ((bf16[1,3584,4]{2,0,1:T(2,128)(2,1)}), bf16[1,3584,4]{2,0,1:T(2,128)(2,1)}, u32[]{:S(2)}, u32[]{:S(2)}) async-start(bf16[1,3584,4]{2,0,1:T(2,128)(2,1)} %copy.112), calls=%async_computation | async-start | bytes 3670016 | tf_op jit(solution)/shard_map/all_to_all | solution.py:169
  352.3 44.0 %all-to-all-done = bf16[1,3584,4]{2,0,1:T(2,128)(2,1)} async-done(((bf16[1,3584,4]{2,0,1:T(2,128)(2,1)}), bf16[1,3584,4]{2,0,1:T(2,128)(2,1)}, u32[]{:S(2)}, u32[]{:S(2)}) %all-to-all-start) | async-done | bytes 28704 | tf_op jit(solution)/shard_map/all_to_all | solution.py:169
  396.9 6.0 %all-to-all-start.4 = ((f32[64,1,1]{2,1,0:T(1,128)}), f32[64,1,1]{2,1,0:T(1,128)S(1)}, u32[]{:S(2)}, u32[]{:S(2)}) async-start(f32[64,1,1]{2,1,0:T(1,128)} %broadcast_in_dim.36), calls=%async_computation.4 | async-start | bytes 65536 | tf_op jit(solution)/shard_map/all_to_all | solution.py:55
  403.0 1.8 copy.127
  404.7 1.3 reshape.292
  406.0 1.8 copy.130
  408.1 3.7 copy.113
  412.8 1.6 multiply_bitcast_fusion
  414.4 2.8 copy.128
  417.2 1.5 reshape.293
  418.9 1.1 convolution_multiply_fusion.3
  420.0 1.1 convolution_multiply_fusion.2
  (55 shorter events, 6.1 us)
Async XLA Ops:
  7.2 64.2 %copy-start = (bf16[256,3584]{1,0:T(8,128)(2,1)S(1)}, bf16[256,3584]{1,0:T(8,128)(2,1)}, u32[]{:S(2)}) copy-start(bf16[256,3584]{1,0:T(8,128)(2,1)} %param.11) | copy-start | bytes 5505028
  7.2 62.7 %all-gather.6.cloned.1.call-start = ((), (), s32[]{:S(2)}) async-start(), calls=%async_computation.6 | async-start | bytes 3612672 | tf_op jit(solution)/shard_map/all_gather | solution.py:31
  20.2 51.2 %copy-start.4 = (bf16[3584,128]{1,0:T(8,128)(2,1)S(1)}, bf16[3584,128]{1,0:T(8,128)(2,1)}, u32[]{:S(2)}) copy-start(bf16[3584,128]{1,0:T(8,128)(2,1)} %param.14) | copy-start | bytes 2752516
  20.3 73.3 %all-gather.8.cloned.1.call-start = ((), (), s32[]{:S(2)}) async-start(), calls=%async_computation.7 | async-start | bytes 9633792 | tf_op jit(solution)/shard_map/all_gather | solution.py:31
  69.9 107.9 %all-gather.10.cloned.1.call-start = ((), (), s32[]{:S(2)}) async-start(), calls=%async_computation.8 | async-start | bytes 6522880 | tf_op jit(solution)/shard_map/all_gather | solution.py:152
  96.9 2.2 copy-start.9
  96.9 2.2 copy-start.11
  106.1 1.4 copy-start.6
  106.1 1.4 copy-start.7
  108.1 1.3 copy-start.2
  108.2 1.9 copy-start.13
  110.0 2.6 copy-start.12
  112.8 70.0 %copy-start.8 = (bf16[1,4,3584]{2,1,0:T(4,128)(2,1)S(1)}, bf16[1,4,3584]{2,1,0:T(4,128)(2,1)}, u32[]{:S(2)}) copy-start(bf16[1,4,3584]{2,1,0:T(4,128)(2,1)} %param.20) | copy-start | bytes 86020
  190.7 27.1 %all-to-all-start.1 = ((bf16[4,1,256,896]{3,2,1,0:T(8,128)(2,1)}), bf16[4,1,256,896]{3,2,1,0:T(8,128)(2,1)S(1)}, u32[]{:S(2)}, u32[]{:S(2)}) async-start(bf16[4,1,256,896]{3,2,1,0:T(8,128)(2,1)} %bitcast.98), calls=%async_computation.1 | async-start | bytes 3670016 | tf_op jit(solution)/shard_map/all_to_all | solution.py:49
  194.7 23.3 %copy-start.5 = (bf16[256,896]{1,0:T(8,128)(2,1)S(1)}, bf16[256,896]{1,0:T(8,128)(2,1)}, u32[]{:S(2)}) copy-start(bf16[256,896]{1,0:T(8,128)(2,1)} %param.12) | copy-start | bytes 1376260
  227.9 64.2 %all-to-all-start.3 = ((f32[64,1,1]{2,1,0:T(1,128)}), f32[64,1,1]{2,1,0:T(1,128)S(1)}, u32[]{:S(2)}, u32[]{:S(2)}) async-start(f32[64,1,1]{2,1,0:T(1,128)} %broadcast_in_dim.35), calls=%async_computation.3 | async-start | bytes 65536 | tf_op jit(solution)/shard_map/all_to_all | solution.py:55
  292.2 52.6 %all-to-all-start.5 = ((bf16[1,4,3584]{1,0,2:T(2,128)(2,1)}), bf16[1,4,3584]{1,0,2:T(2,128)(2,1)S(1)}, u32[]{:S(2)}, u32[]{:S(2)}) async-start(bf16[1,4,3584]{1,0,2:T(2,128)(2,1)} %copy.129), calls=%async_computation.5 | async-start | bytes 3670016 | tf_op jit(solution)/shard_map/all_to_all | solution.py:170
  299.4 2.1 copy-start.10
  344.8 51.5 %all-to-all-start = ((bf16[1,3584,4]{2,0,1:T(2,128)(2,1)}), bf16[1,3584,4]{2,0,1:T(2,128)(2,1)}, u32[]{:S(2)}, u32[]{:S(2)}) async-start(bf16[1,3584,4]{2,0,1:T(2,128)(2,1)} %copy.112), calls=%async_computation | async-start | bytes 3670016 | tf_op jit(solution)/shard_map/all_to_all | solution.py:169
  396.9 15.3 %all-to-all-start.4 = ((f32[64,1,1]{2,1,0:T(1,128)}), f32[64,1,1]{2,1,0:T(1,128)S(1)}, u32[]{:S(2)}, u32[]{:S(2)}) async-start(f32[64,1,1]{2,1,0:T(1,128)} %broadcast_in_dim.36), calls=%async_computation.4 | async-start | bytes 65536 | tf_op jit(solution)/shard_map/all_to_all | solution.py:55
  407.9 4.9 %copy-start.3 = (f32[64,3584]{0,1:T(8,128)S(1)}, f32[64,3584]{0,1:T(8,128)}, u32[]{:S(2)}) copy-start(f32[64,3584]{0,1:T(8,128)} %copy.127) | copy-start | bytes 2752516
  414.3 6.7 %copy-start.1 = (bf16[256,3584]{1,0:T(8,128)(2,1)S(1)}, bf16[256,3584]{1,0:T(8,128)(2,1)}, u32[]{:S(2)}) copy-start(bf16[256,3584]{1,0:T(8,128)(2,1)} %param.11) | copy-start | bytes 5505028
Sparse Core Ops, SparseCore 0:
  20.4 49.4 all-gather.5
  71.7 21.7 all-gather.7
  96.2 81.5 all-gather.9
where the time goes:
time: 430 us; the launch traced here: 429 us
  waiting for transfers between devices  241 us (56%)
  blocking collectives  71.3 us (17%)
  local copies, waits for them, and re-layouts  38.2 us (9%)
  starting transfers between devices  31.5 us (7%)
  matrix products  18.6 us (4%)
  between operations  17.9 us (4%)
  other arithmetic  10.5 us (2%)
    all_gather x2, waiting for transfers between devices, all_blocks(): parts = lax.all_gather(parts, axes[k], axis=0, tiled=True)  69.5 us
    all_gather x1, waiting for transfers between devices, per_device(): lax.all_gather(w_out, POP, axis=1, tiled=True)  65.1 us
    all_gather x1, blocking collectives, side_by_side(): result, at, done = (lax.all_gather(both, axis, axis=dim, tiled=True), 0, [])  51.8 us
    all_to_all x1, waiting for transfers between devices, per_device(): lax.all_to_all(query_left_factors, POP, split_axis=1, concat_axis=0, tile...  44 us
    all_to_all x1, waiting for transfers between devices, per_device(): lax.all_to_all(o_right, POP, split_axis=2, concat_axis=0, tiled=True)  38.7 us
    all_to_all x1, waiting for transfers between devices, summed_on_arrival(): lax.all_to_all(cut_along(shard, dim, devices), axis, 0, 0, tiled=True)  22.5 us
    all_to_all x2, starting transfers between devices, copy_for_each(): return lax.all_to_all(copies, axis, split_axis=0, concat_axis=0, tiled=True)  14 us
    all_gather x1, blocking collectives, all_blocks(): parts = lax.all_gather(parts, axes[k], axis=0, tiled=True)  13 us
  transfers between devices with their start and end apart: 8, of which 7 were waited for; matrix products, arithmetic and copies ran while one was open for 9% of the time, Pallas kernels for 0%

commit v1 on v0

v1 whole, which is shorter than its diff:
```python
import functools
import math

import jax
import jax.numpy as jnp
from jax import lax
from jax.experimental import pallas as pl
from jax.experimental.pallas import tpu as pltpu
from jax.sharding import Mesh
from jax.sharding import PartitionSpec as P

D = 3584
HEADS = 28
KV_HEADS = 4
HEAD_DIM = 128
RANK = 4
POP = ("pop_0", "pop_1", "pop_2")
CHIPS = ("pop_0", "pop_1")

noise_scale = 0.5
rope_base = 1000000.0
spread_floor = 0.001

F32 = jnp.float32
BF16 = jnp.bfloat16
NT = (((1,), (1,)), ((), ()))
TN = (((0,), (0,)), ((), ()))


def vmem(n):
    return [pl.BlockSpec(memory_space=pltpu.VMEM)] * n


def iota(shape, dim):
    return lax.broadcasted_iota(jnp.int32, shape, dim)


def shift(x, axis, size, step):
    return lax.ppermute(x, axis, [(i, (i + step) % size) for i in range(size)])


def swap(x):
    return lax.ppermute(x, "pop_2", [(0, 1), (1, 0)])


def tables(position, head_size):
    index = jnp.arange(head_size // 2, dtype=F32)
    freq = jnp.exp(-math.log(rope_base) * 2.0 * index / head_size)
    angle = position[:, None] * freq[None, :]
    c, s = jnp.cos(angle), jnp.sin(angle)
    return jnp.concatenate([c, c], axis=-1), jnp.concatenate([-s, s], axis=-1)


def attention_kernel(heads, first_ref, recv_ref, base_ref, keys_ref, values_ref, cos_ref, sin_ref, mixed_ref, low_ref):
    tok = keys_ref.shape[0]
    rows = 256
    scale = HEAD_DIM ** (-0.5)
    small = recv_ref[:, :, 896:1024].astype(F32).reshape(rows, 128).astype(BF16)
    lane = iota((128, rows), 1)
    pick = (iota((128, rows), 0) == 112 + (lane & 3)).astype(BF16)
    spread = jnp.dot(small, pick, preferred_element_type=F32)
    r, c = iota((rows, rows), 0), iota((rows, rows), 1)
    mine = (r >> 3) == (c >> 3)
    upper = (c & 7) < 4
    left = [
        jnp.where(mine & upper, spread, 0.0).astype(BF16),
        jnp.where(mine & ~upper, spread, 0.0).astype(BF16),
    ]
    right = recv_ref[:, :, 1024:1536].astype(F32).reshape(rows, 512).astype(BF16)
    low = [jnp.dot(a, right, preferred_element_type=F32) for a in left]
    cos = jnp.broadcast_to(cos_ref[...][None], (rows // 8, 8, 128)).reshape(rows, 128)
    sin = jnp.broadcast_to(sin_ref[...][None], (rows // 8, 8, 128)).reshape(rows, 128)
    keys, values = keys_ref[...], values_ref[...]
    seen = (iota((rows, tok), 0) & 7) + first_ref[0] >= iota((rows, tok), 1)
    for h in range(heads):
        part = low[h // 4][:, (h % 4) * 128 : (h % 4 + 1) * 128]
        base = base_ref[:, h * 128 : (h + 1) * 128]
        q = jnp.broadcast_to(base[None], (rows // 8, 8, 128)).reshape(rows, 128) + part
        q = (q * cos + pltpu.roll(q, 64, 1) * sin).astype(BF16)
        s = lax.dot_general(q, keys, NT, preferred_element_type=F32) * scale
        s = jnp.where(seen, s, -1e30)
        e = jnp.exp(s - jnp.max(s, axis=1, keepdims=True))
        p = (e / jnp.sum(e, axis=1, keepdims=True)).astype(BF16)
        mixed_ref[:, h * 128 : (h + 1) * 128] = jnp.dot(p, values, preferred_element_type=F32).astype(BF16)
    o_left = recv_ref[:, :, 1536:2048].astype(F32).reshape(rows, 512).astype(BF16)
    d1 = lax.dot_general(o_left, mixed_ref[:, :512], NT, preferred_element_type=F32)
    d2 = lax.dot_general(o_left[:, :384], mixed_ref[:, 512:896], NT, preferred_element_type=F32)
    d = jnp.where((r & 7) < 4, d1, d2)
    d = jnp.where(mine, d, 0.0).reshape(rows // 8, 8, rows)
    d = jnp.sum(d, axis=0)
    hi = d.astype(BF16).astype(F32)
    low_ref[...] = jnp.stack([hi, d - hi], axis=0)


def project_kernel(where_ref, *refs):
    *pieces, mixed_a, mixed_b, low_a, low_b, out_ref = refs
    shapes = [(0, 4), (1, 4), (2, 4), (3, 4), (4, 4), (5, 4), (6, 4), (7, 2), (7, 2)]
    a, b = mixed_a[...], mixed_b[...]
    done = 0
    for ref, (e, n) in zip(pieces, shapes):
        w = ref[...].astype(F32).reshape(n * 64, 896).astype(BF16)
        first = done if n == 2 else 0
        z = where_ref[4 + e]
        ra = lax.dot_general(w, a, NT, preferred_element_type=F32)
        rb = lax.dot_general(w, b, NT, preferred_element_type=F32)
        for i in range(n):
            j = where_ref[first + i]
            out_ref[j, pl.ds(z * 7, 7), :, 0:256] = ra[i * 64 : i * 64 + 56].reshape(7, 8, 256).astype(BF16)
            out_ref[j, pl.ds(z * 7, 7), :, 256:512] = rb[i * 64 : i * 64 + 56].reshape(7, 8, 256).astype(BF16)
        if n == 2:
            done = 2
    for j in range(4):
        out_ref[j, 56:58, :, 0:256] = low_a[...].astype(BF16)
        out_ref[j, 56:58, :, 256:512] = low_b[...].astype(BF16)


def error_kernel(recv_ref, right_ref, owner_ref, target_ref, err_ref):
    total = recv_ref[0, :56].astype(F32)
    low = recv_ref[0, 56:58].astype(F32)
    for j in range(1, 4):
        total = total + recv_ref[j, :56].astype(F32)
        low = low + recv_ref[j, 56:58].astype(F32)
    total = total.reshape(448, 512)
    low = low[0] + low[1]
    low = low[0:4] + low[4:8]
    low = jnp.concatenate([low, low], axis=0)
    low = jnp.broadcast_to(low[None], (32, 8, 512)).reshape(256, 512)
    r, c = iota((256, 512), 0), iota((256, 512), 1)
    mine = (owner_ref[...] == ((c & 255) >> 3)) & (((r & 7) >> 2) == (c >> 8))
    low = jnp.where(mine, low, 0.0)
    right = right_ref[...]
    for _ in range(3):
        piece = low.astype(BF16)
        total = total + lax.dot_general(right, piece, TN, preferred_element_type=F32)
        low = low - piece.astype(F32)
    tile = (iota((8, 512), 0) == (iota((8, 512), 1) & 7)).astype(BF16)
    target = lax.dot_general(target_ref[...], tile, TN, preferred_element_type=F32)
    diff = total - target
    err_ref[...] = jnp.sum((diff * diff).reshape(56, 8, 512), axis=0)


def call(kernel, out, args, name, smem=0, flops=10**9):
    return pl.pallas_call(
        kernel,
        out_shape=out,
        in_specs=[pl.BlockSpec(memory_space=pltpu.SMEM)] * smem + vmem(len(args) - smem),
        out_specs=jax.tree.map(lambda _: pl.BlockSpec(memory_space=pltpu.VMEM), out),
        name=name,
        cost_estimate=pl.CostEstimate(flops=flops, bytes_accessed=2 * 10**6, transcendentals=0),
        compiler_params=pltpu.CompilerParams(vmem_limit_bytes=40 * 2**20),
    )(*args)


def per_device(
    tokens,
    target,
    w_query,
    w_key,
    w_value,
    w_out,
    query_left_factors,
    query_right_factors,
    o_left,
    o_right,
    member_ids,
):
    tok = tokens.shape[0]
    feats = w_query.shape[1]
    heads = feats // HEAD_DIM
    x, z, c = (lax.axis_index(a) for a in POP)
    y = lax.axis_index("mp")
    k = x * 8 + z
    p = 2 * k + c
    sign = (1 - 2 * (member_ids[0] % 2)).astype(F32)
    half = (noise_scale * sign).astype(BF16)
    twice = (sign / noise_scale).astype(BF16)

    o_r = o_right[0]
    o_cut = lax.dynamic_slice(o_r, (0, feats * y), (RANK, feats)).reshape(RANK, 8, 2, 56)
    o_cut = jnp.moveaxis(o_cut, 2, 0).reshape(2, RANK, 448)
    o_cut = jnp.where(c == 0, o_cut, o_cut[::-1]).reshape(8, 448) * half
    piece = jnp.concatenate([w_out.T, jnp.pad(o_cut, ((0, 0), (0, 448)))], axis=0)
    xs = [piece, shift(piece, "pop_0", 4, 1), shift(piece, "pop_0", 4, 2), shift(piece, "pop_0", 4, 3)]
    block = jnp.stack(xs)
    up1, dn1 = shift(block, "pop_1", 8, 1), shift(block, "pop_1", 8, 7)
    up2, dn2 = shift(up1, "pop_1", 8, 1), shift(dn1, "pop_1", 8, 7)
    up3, dn3 = shift(up2, "pop_1", 8, 1), shift(dn2, "pop_1", 8, 7)
    up4, dn4 = shift(up3[:2], "pop_1", 8, 1), shift(dn3[2:], "pop_1", 8, 7)
    pieces = [block, up1, dn1, up2, dn2, up3, dn3, up4, dn4]
    z_of = jnp.stack([(z - e) % 8 for e in (0, 1, -1, 2, -2, 3, -3, 4)])
    x_of = jnp.stack([(x - d) % 4 for d in range(4)])
    where = jnp.concatenate([x_of, z_of]).astype(jnp.int32)

    rows = lax.dynamic_slice(tokens, (0, 56 * p), (tok, 56))
    share = jnp.dot(rows, w_query, preferred_element_type=F32).astype(BF16).reshape(32, 8, feats)
    low_q = jnp.dot(tokens, query_left_factors[0], preferred_element_type=F32).astype(BF16) * half
    low_q = low_q.reshape(32, 8, RANK)
    cut_q = jnp.moveaxis((query_left_factors[0].T * twice).reshape(RANK, 32, 112), 1, 0)
    cut_o = jnp.moveaxis((o_r * twice).reshape(RANK, 32, 112), 1, 0)
    small = jnp.concatenate([cut_q, cut_o], axis=1)
    small = jnp.concatenate([small, low_q, jnp.zeros((32, 8, 12), BF16)], axis=2)

    def folded(a):
        return jnp.concatenate([a[:, :512], jnp.pad(a[:, 512:], ((0, 0), (0, 128)))], axis=0)

    both = jnp.concatenate([folded(query_right_factors[0]), folded(o_left[0].T)], axis=1)
    sent = jnp.concatenate([share, small, jnp.broadcast_to(both[None], (32, 8, 1024))], axis=2)
    recv = lax.all_to_all(sent, CHIPS, 0, 0, tiled=True)

    cos_all, sin_all = tables(jnp.arange(tok, dtype=F32), HEAD_DIM)
    k32 = jnp.dot(tokens, w_key, preferred_element_type=F32)
    keys = (k32 * cos_all + jnp.roll(k32, 64, axis=1) * sin_all).astype(BF16)
    values = jnp.dot(tokens, w_value, preferred_element_type=F32).astype(BF16)
    cos8, sin8 = tables((k * 8).astype(F32) + jnp.arange(8, dtype=F32), HEAD_DIM)

    half_base = jnp.sum(recv[:, :, :feats].astype(F32), axis=0)
    base = half_base + swap(half_base)
    mixed, low = call(
        functools.partial(attention_kernel, heads),
        (jax.ShapeDtypeStruct((256, feats), BF16), jax.ShapeDtypeStruct((2, 8, 256), F32)),
        ((k * 8).astype(jnp.int32).reshape(1), recv, base, keys, values, cos8, sin8),
        "attention",
        smem=1,
    )
    mixed_b, low_b = swap(mixed), swap(low)

    factors = recv[:, :, 1024:2048]
    factors_b = swap(factors)
    narrow = recv[:, :, 896:1008].reshape(32, 2, RANK, 2, 56)
    narrow = jnp.moveaxis(narrow, 3, 0)
    narrow = jnp.where(c == 0, narrow, narrow[::-1])
    narrow_b = swap(narrow[1])

    def unfolded(a, b, at):
        both = jnp.stack([a[:, :, at : at + 512], b[:, :, at : at + 512]])
        full = jnp.concatenate([both[:, :, :4], both[:, :, 4:, :384]], axis=3)
        return full.reshape(256, feats).astype(F32)

    right_q = unfolded(factors, factors_b, 0)
    right_o = unfolded(factors, factors_b, 512)
    left_all = jnp.stack([narrow[0], narrow_b]).astype(F32)

    out = call(
        project_kernel,
        jax.ShapeDtypeStruct((4, 58, 8, 512), BF16),
        (where, *pieces, mixed, mixed_b, low, low_b),
        "project",
        smem=1,
        flops=2 * 10**9,
    )
    met = lax.all_to_all(out, "mp", 0, 0, tiled=True)

    tails = jnp.concatenate([q[:, 56:64, :448] for q in pieces], axis=0)
    right = jnp.concatenate([tails[:, :4], swap(tails[:, 4:])], axis=1).reshape(256, 448)
    owner = (x_of[None, :] * 8 + z_of[:, None]).reshape(32)
    owner = jnp.broadcast_to(jnp.repeat(owner, 8)[:, None], (256, 512)).astype(jnp.int32)
    goal = lax.dynamic_slice(target, (8 * k, 0), (8, feats)).reshape(8, 8, 2, 56)
    goal = jnp.where(c == 0, goal[:, :, 0], goal[:, :, 1]).reshape(8, 448)
    err = call(
        error_kernel,
        jax.ShapeDtypeStruct((8, 512), F32),
        (met, right, owner, goal),
        "error",
    )
    err = jnp.sum(err, axis=0).reshape(2, 256)
    err = jnp.where(c == 0, err, err[::-1]).reshape(1, 512)
    err = lax.all_to_all(jnp.broadcast_to(err[None], (8, 1, 512)), ("pop_2", "mp"), 0, 0, tiled=True)
    err = jnp.sum(err, axis=0)
    err = lax.all_to_all(jnp.broadcast_to(err[None], (32, 1, 512)), CHIPS, 0, 0, tiled=True)
    errors = jnp.sum(jnp.sum(err, axis=(0, 1)).reshape(2, 32, 8), axis=2)
    everyone = -(errors / (tok * D))
    mean = jnp.sum(everyone) / 64
    spread = jnp.sum((everyone - mean) * (everyone - mean)) / 64
    weight = (everyone - mean) / jnp.sqrt(spread + spread_floor)
    weight = jnp.where(c == 0, weight, weight[::-1])
    fitness = lax.dynamic_slice(everyone, (c, k), (1, 1)).reshape(1)
    left = left_all * weight[:, :, None, None, None]
    left_q = left[:, :, 0].reshape(256, 56)
    left_o = left[:, :, 1].reshape(256, 56)
    dot = functools.partial(lax.dot_general, dimension_numbers=TN, precision=lax.Precision.HIGHEST)
    grad_query = dot(left_q, right_q)
    grad_out = dot(left_o, right_o).T
    return (grad_query, grad_out, fitness)


def solution(mesh):
    torus = Mesh(mesh.devices.reshape(4, 8, 2, mesh.shape["mp"]), ("pop_0", "pop_1", "pop_2", "mp"))
    placed = (
        P(),
        P(None, "mp"),
        P(POP, "mp"),
        P(None, "mp"),
        P(None, "mp"),
        P("mp", POP),
        P(POP, None, None),
        P(POP, None, "mp"),
        P(POP, "mp", None),
        P(POP, None, None),
        P(POP),
    )
    return jax.shard_map(
        per_device,
        mesh=torus,
        in_specs=placed,
        out_specs=(P(POP, "mp"), P("mp", POP), P(POP)),
        check_vma=False,
    )
```

time: 430 us -> 174 us (0.40)
  waiting for transfers between devices: 241 us -> 68 us
  blocking collectives: 71.3 us -> 0 us
  starting transfers between devices: 31.5 us -> 46.7 us
  between operations: 17.9 us -> 3.37 us
  local copies, waits for them, and re-layouts: 38.2 us -> 23.7 us
  matrix products: 18.6 us -> 7.36 us
  Pallas kernels: 0 us -> 9.72 us
    all_gather x3 -> x0, waiting for transfers between devices: 135 us -> none  [the longest x2 69.5 us: all_blocks(): parts = lax.all_gather(parts, axes[k], axis=0, tiled=True)]
    all_to_all x5 -> x4, waiting for transfers between devices: 105 us -> 27.7 us  [the longest x1 19.5 us: per_device(): met = lax.all_to_all(out, 'mp', 0, 0, tiled=True)]
    all_gather x2 -> x0, blocking collectives: 64.8 us -> none  [the longest x1 51.8 us: side_by_side(): result, at, done = (lax.all_gather(both, axis, axis=dim, tiled=True), 0, [])]
    ppermute x0 -> x17, waiting for transfers between devices: none -> 40.3 us  [the longest x11 38 us: shift(): return lax.ppermute(x, axis, [(i, (i + step) % size) for i in range(size)])]
    ppermute x0 -> x17, starting transfers between devices: none -> 21.9 us  [the longest x11 16.5 us: shift(): return lax.ppermute(x, axis, [(i, (i + step) % size) for i in range(size)])]
    dot_general x10 -> x6, matrix products: 18.6 us -> 7.36 us  [the longest x1 1.8 us: per_device(): k32 = jnp.dot(tokens, w_key, preferred_element_type=F32)]
    pallas_call x0 -> x3, Pallas kernels: none -> 9.72 us  [call(): pl.pallas_call(kernel, out_shape=out, in_specs=[pl.BlockSpec(memory_space...]
    all_to_all x5 -> x4, starting transfers between devices: 31.4 us -> 24.7 us  [the longest x1 8.61 us: per_device(): recv = lax.all_to_all(sent, CHIPS, 0, 0, tiled=True)]
  transfers between devices with their start and end apart: 8 -> 21, of which waited for: 7 -> 8; matrix products, arithmetic and copies ran while one was open for 9% -> 21% of each run, Pallas kernels for 0% -> 3%
where the time goes in v1:
time: 174 us; the launch traced here: 172 us
  waiting for transfers between devices  68 us (39%)
  starting transfers between devices  46.7 us (27%)
  local copies, waits for them, and re-layouts  23.7 us (14%)
  other arithmetic  13.1 us (8%)
  Pallas kernels  9.72 us (6%)
  matrix products  7.36 us (4%)
  between operations  3.37 us (2%)
    ppermute x11, waiting for transfers between devices, shift(): return lax.ppermute(x, axis, [(i, (i + step) % size) for i in range(size)])  38 us
    all_to_all x1, waiting for transfers between devices, per_device(): met = lax.all_to_all(out, 'mp', 0, 0, tiled=True)  19.5 us
    ppermute x11, starting transfers between devices, shift(): return lax.ppermute(x, axis, [(i, (i + step) % size) for i in range(size)])  16.5 us
    pallas_call x3, Pallas kernels, call(): pl.pallas_call(kernel, out_shape=out, in_specs=[pl.BlockSpec(memory_space...  9.72 us
    all_to_all x1, starting transfers between devices, per_device(): recv = lax.all_to_all(sent, CHIPS, 0, 0, tiled=True)  8.61 us
    unnamed x31, local copies, waits for them, and re-layouts  7.71 us
    all_to_all x1, starting transfers between devices, per_device(): lax.all_to_all(jnp.broadcast_to(err[None], (32, 1, 512)), CHIPS, 0, 0, ti...  7.35 us
    all_to_all x1, waiting for transfers between devices, per_device(): lax.all_to_all(jnp.broadcast_to(err[None], (32, 1, 512)), CHIPS, 0, 0, ti...  5.5 us
  transfers between devices with their start and end apart: 21, of which 8 were waited for; matrix products, arithmetic and copies ran while one was open for 21% of the time, Pallas kernels for 3%

profile of v1, /device:TPU:1, one launch (start us, length us, event | category | flops | bytes accessed | tf_op | source)
XLA Modules:
  0.0 172.0 jit_solution(13940637715842121669)
XLA Ops:
  2.4 1.6 fusion.29
  4.0 2.0 %collective-permute-start.1 = (bf16[64,896]{1,0:T(8,128)(2,1)}, bf16[64,896]{1,0:T(8,128)(2,1)}, u32[]{:S(2)}, u32[]{:S(2)}) collective-permute-start(bf16[64,896]{1,0:T(8,128)(2,1)} %get-tuple-element.20), channel_id=1, source_target_pairs={{0,64},{64,128},{128,192},{192,0},{1,65},{65,129},{129,193},{193,1... | collective-permute-start | bytes 344072 | tf_op jit(solution)/shard_map/ppermute | solution.py:39
  6.0 2.5 %collective-permute-start.2 = (bf16[64,896]{1,0:T(8,128)(2,1)}, bf16[64,896]{1,0:T(8,128)(2,1)}, u32[]{:S(2)}, u32[]{:S(2)}) collective-permute-start(bf16[64,896]{1,0:T(8,128)(2,1)} %get-tuple-element.20), channel_id=1, source_target_pairs={{0,128},{64,192},{128,0},{192,64},{1,129},{65,193},{129,1},{193,65... | collective-permute-start | bytes 344072 | tf_op jit(solution)/shard_map/ppermute | solution.py:39
  8.5 1.2 collective-permute-start.3
  12.4 0.8 broadcast_multiply_fusion
  13.3 0.8 fusion.22
  14.1 1.3 fusion.1
  16.2 2.0 %concatenate.58 = bf16[32,8,2048]{2,1,0:T(8,128)(2,1)} concatenate(bf16[32,8,896]{2,1,0:T(8,128)(2,1)S(1)} %fusion, bf16[32,8,112]{2,1,0:T(8,128)(2,1)S(1)} %pad_maximum_fusion.3, bf16[32,8,4]{2,1,0:T(8,128)(2,1)S(1)} %bitcast.80, bf16[32,8,12]{2,1,0:T(8,128)(2,1)S(1)} %broadcast_in_dim.16, bf16[32,8,1024]{2,1,0:T(8,128)(2,1)S(1)} %broadcast_in_dim.17), dimensions={2} | concatenate | bytes 2097152 | tf_op jit(solution)/shard_map/concatenate | solution.py:207
  18.2 8.6 %all-to-all-start = ((bf16[32,8,2048]{2,1,0:T(8,128)(2,1)}), bf16[32,8,2048]{2,1,0:T(8,128)(2,1)S(1)}, u32[]{:S(2)}, u32[]{:S(2)}) async-start(bf16[32,8,2048]{2,1,0:T(8,128)(2,1)} %concatenate.58), calls=%async_computation | async-start | bytes 2097152 | tf_op jit(solution)/shard_map/all_to_all | solution.py:208
  27.5 1.8 %fusion.34 = f32[256,128]{1,0:T(8,128)S(1)} fusion(bf16[256,3584]{1,0:T(8,128)(2,1)S(1)} %copy-done, bf16[3584,128]{1,0:T(8,128)(2,1)} %param.14), kind=kOutput, calls=%fused_computation.92 | convolution fusion | flops 234881024 | bytes 2883584 | tf_op jit(solution)/shard_map/dot_general | solution.py:211
  29.3 0.8 fusion.32
  30.1 1.1 fusion.8.keys_ref
  31.4 1.1 pad_maximum_fusion.2.refs_0_
  32.6 1.3 collective-permute-start.4
  33.9 1.4 collective-permute-start.5
  36.1 1.8 %convolution_convert_fusion.1.values_ref = bf16[256,128]{1,0:T(8,128)(2,1)S(1)} fusion(bf16[256,3584]{1,0:T(8,128)(2,1)S(1)} %copy-done, bf16[3584,128]{1,0:T(8,128)(2,1)} %param.15), kind=kOutput, calls=%fused_computation.2 | convolution fusion | flops 234913792 | bytes 2818048 | tf_op jit(solution)/shard_map/dot_general | solution.py:213
  37.9 23.8 %collective-permute-done.4.refs_1_ = bf16[4,64,896]{2,1,0:T(8,128)(2,1)} collective-permute-done((bf16[4,64,896]{2,1,0:T(8,128)(2,1)S(1)}, bf16[4,64,896]{2,1,0:T(8,128)(2,1)}, u32[]{:S(2)}, u32[]{:S(2)}) %collective-permute-start.4) | collective-permute-done | bytes 458784 | tf_op jit(solution)/shard_map/ppermute | solution.py:39
  61.8 2.7 %collective-permute-start.7 = (bf16[4,64,896]{2,1,0:T(8,128)(2,1)}, bf16[4,64,896]{2,1,0:T(8,128)(2,1)}, u32[]{:S(2)}, u32[]{:S(2)}) collective-permute-start(bf16[4,64,896]{2,1,0:T(8,128)(2,1)} %collective-permute-done.5.refs_2_), channel_id=1, source_target_pairs={{0,56},{8,0},{16,8},{24,16},{32,24},{40,32},{48,40},{56,48},{1,57}... | collective-permute-start | bytes 1376264 | tf_op jit(solution)/shard_map/ppermute | solution.py:39
  65.0 0.8 slice_dynamic-update-slice_fusion.5
  65.7 8.0 %collective-permute-done.6.refs_3_ = bf16[4,64,896]{2,1,0:T(8,128)(2,1)} collective-permute-done((bf16[4,64,896]{2,1,0:T(8,128)(2,1)}, bf16[4,64,896]{2,1,0:T(8,128)(2,1)}, u32[]{:S(2)}, u32[]{:S(2)}) %collective-permute-start.6) | collective-permute-done | bytes 458784 | tf_op jit(solution)/shard_map/ppermute | solution.py:39
  73.8 2.7 %collective-permute-start.9 = (bf16[4,64,896]{2,1,0:T(8,128)(2,1)}, bf16[4,64,896]{2,1,0:T(8,128)(2,1)S(1)}, u32[]{:S(2)}, u32[]{:S(2)}) collective-permute-start(bf16[4,64,896]{2,1,0:T(8,128)(2,1)} %collective-permute-done.7.refs_4_), channel_id=1, source_target_pairs={{0,56},{8,0},{16,8},{24,16},{32,24},{40,32},{48,40},{56,48},{1,57}... | collective-permute-start | bytes 1376264 | tf_op jit(solution)/shard_map/ppermute | solution.py:39
  76.5 0.8 slice_dynamic-update-slice_fusion.4
  78.7 6.1 %collective-permute-done.8.refs_5_ = bf16[4,64,896]{2,1,0:T(8,128)(2,1)S(1)} collective-permute-done((bf16[4,64,896]{2,1,0:T(8,128)(2,1)}, bf16[4,64,896]{2,1,0:T(8,128)(2,1)S(1)}, u32[]{:S(2)}, u32[]{:S(2)}) %collective-permute-start.8) | collective-permute-done | bytes 458784 | tf_op jit(solution)/shard_map/ppermute | solution.py:39
  86.5 2.8 %collective-permute-start.11 = (bf16[2,64,896]{2,1,0:T(8,128)(2,1)}, bf16[2,64,896]{2,1,0:T(8,128)(2,1)}, u32[]{:S(2)}, u32[]{:S(2)}) collective-permute-start(bf16[2,64,896]{2,1,0:T(8,128)(2,1)} %slice.156), channel_id=1, source_target_pairs={{0,56},{8,0},{16,8},{24,16},{32,24},{40,32},{48,40},{56,48},{1,57}... | collective-permute-start | bytes 688136 | tf_op jit(solution)/shard_map/ppermute | solution.py:39
  89.4 3.9 %collective-permute-start.12 = (f32[8,896]{1,0:T(8,128)S(1)}, f32[8,896]{1,0:T(8,128)S(1)}, u32[]{:S(2)}, u32[]{:S(2)}) collective-permute-start(f32[8,896]{1,0:T(8,128)S(1)} %convert_reduce_fusion), channel_id=1, source_target_pairs={{0,4},{4,0},{1,5},{5,1},{2,6},{6,2},{3,7},{7,3},{8,12},{12,8},{9,1... | collective-permute-start | bytes 86024 | tf_op jit(solution)/shard_map/ppermute | solution.py:43
  93.3 1.4 slice_dynamic-update-slice_fusion.1
  94.7 3.2 %attention.1 = (bf16[256,896]{1,0:T(8,128)(2,1)S(1)}, f32[2,8,256]{2,1,0:T(8,128)S(1)}) custom-call(s32[1]{0:T(128)} %bitcast.32.first_ref, bf16[32,8,2048]{2,1,0:T(8,128)(2,1)S(1)} %all-to-all-done.recv_ref, f32[8,896]{1,0:T(8,128)S(1)} %add.130.base_ref, bf16[256,128]{1,0:T(8,128)(2,1)S(1)} %fusion.8.keys_ref, ...), custom_call_target="tpu_custom_call" | custom-call | flops 1000000000 | bytes 2000000 | tf_op jit(solution)/shard_map/attention/pallas_call | solution.py:143
  98.6 1.3 constant_dynamic-update-slice_fusion.1
  100.5 1.3 constant_dynamic-update-slice_fusion
  101.8 4.2 %project.1 = bf16[4,58,8,512]{3,2,1,0:T(8,128)(2,1)S(1)} custom-call(s32[12]{0:T(128)S(1)} %concatenate.59.where_ref, bf16[4,64,896]{2,1,0:T(8,128)(2,1)S(1)} %pad_maximum_fusion.2.refs_0_, bf16[4,64,896]{2,1,0:T(8,128)(2,1)} %collective-permute-done.4.refs_1_, bf16[4,64,896]{2,1,0:T(8,128)(2,1)} %collective-permute-done.5.refs_2_, ...), custom_call_target="tpu_custom_call" | custom-call | flops 2000000000 | bytes 2000000 | tf_op jit(solution)/shard_map/project/pallas_call | solution.py:143
  106.0 1.2 copy-done.1
  107.2 4.6 %all-to-all-start.1 = ((bf16[4,58,8,512]{3,2,1,0:T(8,128)(2,1)}), bf16[4,58,8,512]{3,2,1,0:T(8,128)(2,1)}, u32[]{:S(2)}, u32[]{:S(2)}) async-start(bf16[4,58,8,512]{3,2,1,0:T(8,128)(2,1)} %copy-done.1), calls=%async_computation.1 | async-start | bytes 3801088 | tf_op jit(solution)/shard_map/all_to_all | solution.py:251
  112.3 1.1 collective-permute-done.15
  114.5 1.2 collective-permute-done.16
  115.8 0.8 fusion.4
  116.6 19.5 %all-to-all-done.1.recv_ref = bf16[4,58,8,512]{3,2,1,0:T(8,128)(2,1)} async-done(((bf16[4,58,8,512]{3,2,1,0:T(8,128)(2,1)}), bf16[4,58,8,512]{3,2,1,0:T(8,128)(2,1)}, u32[]{:S(2)}, u32[]{:S(2)}) %all-to-all-start.1) | async-done | bytes 1900576 | tf_op jit(solution)/shard_map/all_to_all | solution.py:251
  136.2 2.3 %error.1 = f32[8,512]{1,0:T(8,128)S(1)} custom-call(bf16[4,58,8,512]{3,2,1,0:T(8,128)(2,1)} %all-to-all-done.1.recv_ref, bf16[256,448]{1,0:T(8,128)(2,1)S(1)} %maximum_bitcast_fusion.right_ref, s32[256,512]{1,0:T(8,128)S(1)} %broadcast_in_dim.20.owner_ref, bf16[8,448]{1,0:T(8,128)(2,1)S(1)} %select_n.138.target_ref), custom_call_target="tpu_custom_call" | custom-call | flops 1000000000 | bytes 2000000 | tf_op jit(solution)/shard_map/error/pallas_call | solution.py:143
  139.2 4.2 %all-to-all-start.2 = ((f32[8,1,512]{2,1,0:T(1,128)}), f32[8,1,512]{2,1,0:T(1,128)S(1)}, u32[]{:S(2)}, u32[]{:S(2)}) async-start(f32[8,1,512]{2,1,0:T(1,128)} %broadcast_in_dim.22), calls=%async_computation.2 | async-start | bytes 32768 | tf_op jit(solution)/shard_map/all_to_all | solution.py:267
  143.4 2.1 %fusion.2 = bf16[2,32,4,896]{3,2,1,0:T(4,128)(2,1)} fusion(bf16[1,32,8,512]{3,2,1,0:T(8,128)(2,1)} %copy-done.7, bf16[1,32,8,512]{3,2,1,0:T(8,128)(2,1)} %copy-done.6, bf16[2,32,4,512]{3,2,1,0:T(4,128)(2,1)} %fusion.4), kind=kLoop, calls=%fused_computation.11 | loop fusion | flops 1376256 | bytes 1245184 | tf_op jit(solution)/shard_map/concatenate | solution.py:236
  145.6 2.7 %all-to-all-done.2 = f32[8,1,512]{2,1,0:T(1,128)S(1)} async-done(((f32[8,1,512]{2,1,0:T(1,128)}), f32[8,1,512]{2,1,0:T(1,128)S(1)}, u32[]{:S(2)}, u32[]{:S(2)}) %all-to-all-start.2) | async-done | bytes 16416 | tf_op jit(solution)/shard_map/all_to_all | solution.py:267
  149.0 7.3 %all-to-all-start.3 = ((f32[32,1,512]{2,1,0:T(1,128)}), f32[32,1,512]{2,1,0:T(1,128)S(1)}, u32[]{:S(2)}, u32[]{:S(2)}) async-start(f32[32,1,512]{2,1,0:T(1,128)} %broadcast_in_dim.46), calls=%async_computation.3 | async-start | bytes 131072 | tf_op jit(solution)/shard_map/all_to_all | solution.py:269
  156.5 1.1 reshape.133
  157.6 1.0 fusion.3
  158.6 1.1 reshape.132
  159.8 5.5 %all-to-all-done.3 = f32[32,1,512]{2,1,0:T(1,128)S(1)} async-done(((f32[32,1,512]{2,1,0:T(1,128)}), f32[32,1,512]{2,1,0:T(1,128)S(1)}, u32[]{:S(2)}, u32[]{:S(2)}) %all-to-all-start.3) | async-done | bytes 65568 | tf_op jit(solution)/shard_map/all_to_all | solution.py:269
  168.1 0.9 convert_multiply_fusion
  169.3 1.1 fusion.36
  170.3 1.1 fusion.35
  (116 shorter events, 16.6 us)
Async XLA Ops:
  0.6 13.5 %copy-start = (bf16[256,3584]{1,0:T(8,128)(2,1)S(1)}, bf16[256,3584]{1,0:T(8,128)(2,1)}, u32[]{:S(2)}) copy-start(bf16[256,3584]{1,0:T(8,128)(2,1)} %param.11) | copy-start | bytes 5505028
  0.6 15.1 %copy-start.10 = (bf16[56,896]{1,0:T(8,128)(2,1)S(1)}, bf16[56,896]{1,0:T(8,128)(2,1)}, u32[]{:S(2)}) copy-start(bf16[56,896]{1,0:T(8,128)(2,1)} %param.13) | copy-start | bytes 301060
  4.0 27.4 %collective-permute-start.1 = (bf16[64,896]{1,0:T(8,128)(2,1)}, bf16[64,896]{1,0:T(8,128)(2,1)}, u32[]{:S(2)}, u32[]{:S(2)}) collective-permute-start(bf16[64,896]{1,0:T(8,128)(2,1)} %get-tuple-element.20), channel_id=1, source_target_pairs={{0,64},{64,128},{128,192},{192,0},{1,65},{65,129},{129,193},{193,1... | collective-permute-start | bytes 344072 | tf_op jit(solution)/shard_map/ppermute | solution.py:39
  6.0 25.4 %collective-permute-start.2 = (bf16[64,896]{1,0:T(8,128)(2,1)}, bf16[64,896]{1,0:T(8,128)(2,1)}, u32[]{:S(2)}, u32[]{:S(2)}) collective-permute-start(bf16[64,896]{1,0:T(8,128)(2,1)} %get-tuple-element.20), channel_id=1, source_target_pairs={{0,128},{64,192},{128,0},{192,64},{1,129},{65,193},{129,1},{193,65... | collective-permute-start | bytes 344072 | tf_op jit(solution)/shard_map/ppermute | solution.py:39
  8.5 22.9 %collective-permute-start.3 = (bf16[64,896]{1,0:T(8,128)(2,1)}, bf16[64,896]{1,0:T(8,128)(2,1)}, u32[]{:S(2)}, u32[]{:S(2)}) collective-permute-start(bf16[64,896]{1,0:T(8,128)(2,1)} %get-tuple-element.20), channel_id=1, source_target_pairs={{0,192},{64,0},{128,64},{192,128},{1,193},{65,1},{129,65},{193,129... | collective-permute-start | bytes 344072 | tf_op jit(solution)/shard_map/ppermute | solution.py:39
  18.2 71.1 %all-to-all-start = ((bf16[32,8,2048]{2,1,0:T(8,128)(2,1)}), bf16[32,8,2048]{2,1,0:T(8,128)(2,1)S(1)}, u32[]{:S(2)}, u32[]{:S(2)}) async-start(bf16[32,8,2048]{2,1,0:T(8,128)(2,1)} %concatenate.58), calls=%async_computation | async-start | bytes 2097152 | tf_op jit(solution)/shard_map/all_to_all | solution.py:208
  32.6 29.2 %collective-permute-start.4 = (bf16[4,64,896]{2,1,0:T(8,128)(2,1)S(1)}, bf16[4,64,896]{2,1,0:T(8,128)(2,1)}, u32[]{:S(2)}, u32[]{:S(2)}) collective-permute-start(bf16[4,64,896]{2,1,0:T(8,128)(2,1)S(1)} %pad_maximum_fusion.2.refs_0_), channel_id=1, source_target_pairs={{0,8},{8,16},{16,24},{24,32},{32,40},{40,48},{48,56},{56,0},{1,9},... | collective-permute-start | bytes 1376264 | tf_op jit(solution)/shard_map/ppermute | solution.py:39
  33.9 27.9 %collective-permute-start.5 = (bf16[4,64,896]{2,1,0:T(8,128)(2,1)S(1)}, bf16[4,64,896]{2,1,0:T(8,128)(2,1)}, u32[]{:S(2)}, u32[]{:S(2)}) collective-permute-start(bf16[4,64,896]{2,1,0:T(8,128)(2,1)S(1)} %pad_maximum_fusion.2.refs_0_), channel_id=1, source_target_pairs={{0,56},{8,0},{16,8},{24,16},{32,24},{40,32},{48,40},{56,48},{1,57}... | collective-permute-start | bytes 1376264 | tf_op jit(solution)/shard_map/ppermute | solution.py:39
  61.8 12.0 %collective-permute-start.6 = (bf16[4,64,896]{2,1,0:T(8,128)(2,1)}, bf16[4,64,896]{2,1,0:T(8,128)(2,1)}, u32[]{:S(2)}, u32[]{:S(2)}) collective-permute-start(bf16[4,64,896]{2,1,0:T(8,128)(2,1)} %collective-permute-done.4.refs_1_), channel_id=1, source_target_pairs={{0,8},{8,16},{16,24},{24,32},{32,40},{40,48},{48,56},{56,0},{1,9},... | collective-permute-start | bytes 1376264 | tf_op jit(solution)/shard_map/ppermute | solution.py:39
  61.8 12.0 %collective-permute-start.7 = (bf16[4,64,896]{2,1,0:T(8,128)(2,1)}, bf16[4,64,896]{2,1,0:T(8,128)(2,1)}, u32[]{:S(2)}, u32[]{:S(2)}) collective-permute-start(bf16[4,64,896]{2,1,0:T(8,128)(2,1)} %collective-permute-done.5.refs_2_), channel_id=1, source_target_pairs={{0,56},{8,0},{16,8},{24,16},{32,24},{40,32},{48,40},{56,48},{1,57}... | collective-permute-start | bytes 1376264 | tf_op jit(solution)/shard_map/ppermute | solution.py:39
  73.8 11.1 %collective-permute-start.8 = (bf16[4,64,896]{2,1,0:T(8,128)(2,1)}, bf16[4,64,896]{2,1,0:T(8,128)(2,1)S(1)}, u32[]{:S(2)}, u32[]{:S(2)}) collective-permute-start(bf16[4,64,896]{2,1,0:T(8,128)(2,1)} %collective-permute-done.6.refs_3_), channel_id=1, source_target_pairs={{0,8},{8,16},{16,24},{24,32},{32,40},{40,48},{48,56},{56,0},{1,9},... | collective-permute-start | bytes 1376264 | tf_op jit(solution)/shard_map/ppermute | solution.py:39
  73.8 11.8 %collective-permute-start.9 = (bf16[4,64,896]{2,1,0:T(8,128)(2,1)}, bf16[4,64,896]{2,1,0:T(8,128)(2,1)S(1)}, u32[]{:S(2)}, u32[]{:S(2)}) collective-permute-start(bf16[4,64,896]{2,1,0:T(8,128)(2,1)} %collective-permute-done.7.refs_4_), channel_id=1, source_target_pairs={{0,56},{8,0},{16,8},{24,16},{32,24},{40,32},{48,40},{56,48},{1,57}... | collective-permute-start | bytes 1376264 | tf_op jit(solution)/shard_map/ppermute | solution.py:39
  78.7 7.6 %copy-start.8 = (bf16[32,8,448]{2,1,0:T(8,128)(2,1)}, bf16[32,8,448]{2,1,0:T(8,128)(2,1)S(1)}, u32[]{:S(2)}) copy-start(bf16[32,8,448]{2,1,0:T(8,128)(2,1)S(1)} %slice_dynamic-update-slice_fusion.2) | copy-start | bytes 688132
  84.8 1.5 copy-start.2
  85.6 13.1 %collective-permute-start.10 = (bf16[2,64,896]{2,1,0:T(8,128)(2,1)}, bf16[2,64,896]{2,1,0:T(8,128)(2,1)}, u32[]{:S(2)}, u32[]{:S(2)}) collective-permute-start(bf16[2,64,896]{2,1,0:T(8,128)(2,1)} %slice.155), channel_id=1, source_target_pairs={{0,8},{8,16},{16,24},{24,32},{32,40},{40,48},{48,56},{56,0},{1,9},... | collective-permute-start | bytes 688136 | tf_op jit(solution)/shard_map/ppermute | solution.py:39
  85.6 0.9 copy-start.4
  86.5 14.0 %collective-permute-start.11 = (bf16[2,64,896]{2,1,0:T(8,128)(2,1)}, bf16[2,64,896]{2,1,0:T(8,128)(2,1)}, u32[]{:S(2)}, u32[]{:S(2)}) collective-permute-start(bf16[2,64,896]{2,1,0:T(8,128)(2,1)} %slice.156), channel_id=1, source_target_pairs={{0,56},{8,0},{16,8},{24,16},{32,24},{40,32},{48,40},{56,48},{1,57}... | collective-permute-start | bytes 688136 | tf_op jit(solution)/shard_map/ppermute | solution.py:39
  89.4 5.3 %collective-permute-start.12 = (f32[8,896]{1,0:T(8,128)S(1)}, f32[8,896]{1,0:T(8,128)S(1)}, u32[]{:S(2)}, u32[]{:S(2)}) collective-permute-start(f32[8,896]{1,0:T(8,128)S(1)} %convert_reduce_fusion), channel_id=1, source_target_pairs={{0,4},{4,0},{1,5},{5,1},{2,6},{6,2},{3,7},{7,3},{8,12},{12,8},{9,1... | collective-permute-start | bytes 86024 | tf_op jit(solution)/shard_map/ppermute | solution.py:43
  94.7 3.4 %copy-start.5 = (bf16[4,64,896]{2,1,0:T(8,128)(2,1)S(1)}, bf16[4,64,896]{2,1,0:T(8,128)(2,1)}, u32[]{:S(2)}) copy-start(bf16[4,64,896]{2,1,0:T(8,128)(2,1)} %copy-done.4) | copy-start | bytes 1376260
  94.7 7.1 %copy-start.3 = (bf16[4,64,896]{2,1,0:T(8,128)(2,1)S(1)}, bf16[4,64,896]{2,1,0:T(8,128)(2,1)}, u32[]{:S(2)}) copy-start(bf16[4,64,896]{2,1,0:T(8,128)(2,1)} %copy-done.2) | copy-start | bytes 1376260
  97.9 3.9 %collective-permute-start.13 = (bf16[256,896]{1,0:T(8,128)(2,1)S(1)}, bf16[256,896]{1,0:T(8,128)(2,1)S(1)}, u32[]{:S(2)}, u32[]{:S(2)}) collective-permute-start(bf16[256,896]{1,0:T(8,128)(2,1)S(1)} %get-tuple-element.5.refs_9_), channel_id=1, source_target_pairs={{0,4},{4,0},{1,5},{5,1},{2,6},{6,2},{3,7},{7,3},{8,12},{12,8},{9,1... | collective-permute-start | bytes 1376264 | tf_op jit(solution)/shard_map/ppermute | solution.py:43
  100.0 1.8 %collective-permute-start.14 = (f32[2,8,256]{2,1,0:T(8,128)S(1)}, f32[2,8,256]{2,1,0:T(8,128)S(1)}, u32[]{:S(2)}, u32[]{:S(2)}) collective-permute-start(f32[2,8,256]{2,1,0:T(8,128)S(1)} %get-tuple-element.6.refs_11_), channel_id=1, source_target_pairs={{0,4},{4,0},{1,5},{5,1},{2,6},{6,2},{3,7},{7,3},{8,12},{12,8},{9,1... | collective-permute-start | bytes 49160 | tf_op jit(solution)/shard_map/ppermute | solution.py:43
  106.0 1.2 copy-start.1
  107.2 4.6 %copy-start.9 = (bf16[32,8,448]{2,1,0:T(8,128)(2,1)S(1)}, bf16[32,8,448]{2,1,0:T(8,128)(2,1)}, u32[]{:S(2)}) copy-start(bf16[32,8,448]{2,1,0:T(8,128)(2,1)} %constant_dynamic-update-slice_fusion) | copy-start | bytes 688132
  107.2 28.8 %all-to-all-start.1 = ((bf16[4,58,8,512]{3,2,1,0:T(8,128)(2,1)}), bf16[4,58,8,512]{3,2,1,0:T(8,128)(2,1)}, u32[]{:S(2)}, u32[]{:S(2)}) async-start(bf16[4,58,8,512]{3,2,1,0:T(8,128)(2,1)} %copy-done.1), calls=%async_computation.1 | async-start | bytes 3801088 | tf_op jit(solution)/shard_map/all_to_all | solution.py:251
  111.9 1.4 collective-permute-start.15
  113.7 2.0 %collective-permute-start.16 = (bf16[32,8,1024]{2,1,0:T(8,128)(2,1)S(1)}, bf16[32,8,1024]{2,1,0:T(8,128)(2,1)S(1)}, u32[]{:S(2)}, u32[]{:S(2)}) collective-permute-start(bf16[32,8,1024]{2,1,0:T(8,128)(2,1)S(1)} %slice.175), channel_id=1, source_target_pairs={{0,4},{4,0},{1,5},{5,1},{2,6},{6,2},{3,7},{7,3},{8,12},{12,8},{9,1... | collective-permute-start | bytes 1572872 | tf_op jit(solution)/shard_map/ppermute | solution.py:43
  114.0 54.1 %collective-permute-start = (bf16[32,2,4,56]{3,0,2,1:T(8,128)(2,1)S(1)}, bf16[32,2,4,56]{3,0,2,1:T(8,128)(2,1)}, u32[]{:S(2)}, u32[]{:S(2)}) collective-permute-start(bf16[32,2,4,56]{3,0,2,1:T(8,128)(2,1)S(1)} %get-tuple-element.18), channel_id=1, source_target_pairs={{0,4},{4,0},{1,5},{5,1},{2,6},{6,2},{3,7},{7,3},{8,12},{12,8},{9,1... | collective-permute-start | bytes 86024 | tf_op jit(solution)/shard_map/ppermute | solution.py:43
  114.5 1.3 copy-start.6
  115.7 0.8 copy-start.7
  139.2 9.1 %all-to-all-start.2 = ((f32[8,1,512]{2,1,0:T(1,128)}), f32[8,1,512]{2,1,0:T(1,128)S(1)}, u32[]{:S(2)}, u32[]{:S(2)}) async-start(f32[8,1,512]{2,1,0:T(1,128)} %broadcast_in_dim.22), calls=%async_computation.2 | async-start | bytes 32768 | tf_op jit(solution)/shard_map/all_to_all | solution.py:267
  149.0 16.2 %all-to-all-start.3 = ((f32[32,1,512]{2,1,0:T(1,128)}), f32[32,1,512]{2,1,0:T(1,128)S(1)}, u32[]{:S(2)}, u32[]{:S(2)}) async-start(f32[32,1,512]{2,1,0:T(1,128)} %broadcast_in_dim.46), calls=%async_computation.3 | async-start | bytes 131072 | tf_op jit(solution)/shard_map/all_to_all | solution.py:269

commit v2 on v1

v2 whole, which is shorter than its diff:
```python
import functools
import math

import jax
import jax.numpy as jnp
from jax import lax
from jax.experimental import pallas as pl
from jax.experimental.pallas import tpu as pltpu
from jax.sharding import Mesh
from jax.sharding import PartitionSpec as P

D = 3584
HEADS = 28
KV_HEADS = 4
HEAD_DIM = 128
RANK = 4
POP = ("pop_0", "pop_1", "pop_2")
CHIPS = ("pop_0", "pop_1")

noise_scale = 0.5
rope_base = 1000000.0
spread_floor = 0.001

F32 = jnp.float32
BF16 = jnp.bfloat16
NT = (((1,), (1,)), ((), ()))
TN = (((0,), (0,)), ((), ()))


def vmem(n):
    return [pl.BlockSpec(memory_space=pltpu.VMEM)] * n


def iota(shape, dim):
    return lax.broadcasted_iota(jnp.int32, shape, dim)


def shift(x, axis, size, step):
    return lax.ppermute(x, axis, [(i, (i + step) % size) for i in range(size)])


def swap(x):
    return lax.ppermute(x, "pop_2", [(0, 1), (1, 0)])


def tables(position, head_size):
    index = jnp.arange(head_size // 2, dtype=F32)
    freq = jnp.exp(-math.log(rope_base) * 2.0 * index / head_size)
    angle = position[:, None] * freq[None, :]
    c, s = jnp.cos(angle), jnp.sin(angle)
    return jnp.concatenate([c, c], axis=-1), jnp.concatenate([-s, s], axis=-1)


def front_kernel(where_ref, tokens_ref, w_ref, left_ref, right_ref, o_ref, out_ref, pad_ref):
    p = where_ref[0]
    start = pl.multiple_of(jnp.minimum((56 * p) // 128 * 128, 3584 - 256), 128)
    at = pl.multiple_of(56 * p - start, 8)
    pad_ref[...] = jnp.zeros_like(pad_ref)
    pad_ref[pl.ds(at, 56), :] = w_ref[...].astype(F32)
    window = tokens_ref[:, pl.ds(start, 256)]
    share = jnp.dot(window, pad_ref[...].astype(BF16), preferred_element_type=F32)
    out_ref[:, :, 0:896] = share.reshape(32, 8, 896).astype(BF16)
    low = lax.dot_general(tokens_ref[...], left_ref[...], NT, preferred_element_type=F32)
    low = low.astype(BF16).astype(F32) * jnp.where(where_ref[1] == 0, 0.5, -0.5)
    out_ref[:, :, 896:1024] = low.reshape(32, 8, 128).astype(BF16)

    def folded(ref):
        a = ref[...].astype(F32)
        b = jnp.concatenate([a[:, 512:896], jnp.zeros((RANK, 128), F32)], axis=1)
        return jnp.broadcast_to(jnp.concatenate([a[:, :512], b], axis=0)[None], (32, 8, 512)).astype(BF16)

    out_ref[:, :, 1024:1536] = folded(right_ref)
    out_ref[:, :, 1536:2048] = folded(o_ref)


def attention_kernel(heads, first_ref, recv_ref, base_ref, other_ref, keys_ref, values_ref, cos_ref, sin_ref, mixed_ref, low_ref):
    tok = keys_ref.shape[0]
    rows = 256
    scale = HEAD_DIM ** (-0.5)
    small = recv_ref[:, :, 896:1024].astype(F32).reshape(rows, 128).astype(BF16)
    lane = iota((128, rows), 1)
    pick = (iota((128, rows), 0) == (lane & 3)).astype(BF16)
    spread = jnp.dot(small, pick, preferred_element_type=F32)
    r, c = iota((rows, rows), 0), iota((rows, rows), 1)
    mine = (r >> 3) == (c >> 3)
    upper = (c & 7) < 4
    left = [
        jnp.where(mine & upper, spread, 0.0).astype(BF16),
        jnp.where(mine & ~upper, spread, 0.0).astype(BF16),
    ]
    right = recv_ref[:, :, 1024:1536].astype(F32).reshape(rows, 512).astype(BF16)
    low = [jnp.dot(a, right, preferred_element_type=F32) for a in left]
    cos = jnp.broadcast_to(cos_ref[...][None], (rows // 8, 8, 128)).reshape(rows, 128)
    sin = jnp.broadcast_to(sin_ref[...][None], (rows // 8, 8, 128)).reshape(rows, 128)
    keys, values = keys_ref[...], values_ref[...]
    seen = (iota((rows, tok), 0) & 7) + first_ref[0] >= iota((rows, tok), 1)
    for h in range(heads):
        part = low[h // 4][:, (h % 4) * 128 : (h % 4 + 1) * 128]
        base = base_ref[:, h * 128 : (h + 1) * 128] + other_ref[:, h * 128 : (h + 1) * 128]
        q = jnp.broadcast_to(base[None], (rows // 8, 8, 128)).reshape(rows, 128) + part
        q = (q * cos + pltpu.roll(q, 64, 1) * sin).astype(BF16)
        s = lax.dot_general(q, keys, NT, preferred_element_type=F32) * scale
        s = jnp.where(seen, s, -1e30)
        e = jnp.exp(s - jnp.max(s, axis=1, keepdims=True))
        p = (e / jnp.sum(e, axis=1, keepdims=True)).astype(BF16)
        mixed_ref[:, h * 128 : (h + 1) * 128] = jnp.dot(p, values, preferred_element_type=F32).astype(BF16)
    o_left = recv_ref[:, :, 1536:2048].astype(F32).reshape(rows, 512).astype(BF16)
    d1 = lax.dot_general(o_left, mixed_ref[:, :512], NT, preferred_element_type=F32)
    d2 = lax.dot_general(o_left[:, :384], mixed_ref[:, 512:896], NT, preferred_element_type=F32)
    d = jnp.where((r & 7) < 4, d1, d2)
    d = jnp.where(mine, d, 0.0).reshape(rows // 8, 8, rows)
    d = jnp.sum(d, axis=0)
    hi = d.astype(BF16).astype(F32)
    low_ref[...] = jnp.stack([hi, d - hi], axis=0)


def project_kernel(split, where_ref, *refs):
    firsts, seconds, (mixed_ref, low_ref), outs, (hold_ref,) = (
        refs[:8],
        refs[8:12],
        refs[12:14],
        refs[14:18],
        refs[18:],
    )
    mixed = mixed_ref[...]
    last = 56 - split

    def times(w, n, rows):
        w = w.astype(F32).reshape(n * rows, 896).astype(BF16)
        return lax.dot_general(w, mixed, NT, preferred_element_type=F32)

    for e, ref in enumerate(firsts):
        got = times(ref[...], 4, split)
        z = where_ref[4 + e]
        for d in range(4):
            hold_ref[where_ref[d], pl.ds(z * 7, split // 8)] = got[d * split : (d + 1) * split].reshape(split // 8, 8, 256).astype(BF16)
    for d, ref in enumerate(seconds):
        got = times(ref[...], 8, last)
        for e in range(8):
            z = where_ref[4 + e]
            hold_ref[where_ref[d], pl.ds(z * 7 + split // 8, last // 8)] = got[e * last : (e + 1) * last].reshape(last // 8, 8, 256).astype(BF16)
    for s, out_ref in enumerate(outs):
        out_ref[0:56] = hold_ref[s]
        out_ref[56:58] = low_ref[...].astype(BF16)


def error_kernel(core_ref, *refs):
    sides, (right_ref, target_ref, err_ref) = (refs[:4], refs[4:8]), refs[8:]
    core = core_ref[0]
    right = right_ref[...]
    tile = (iota((8, 256), 0) == (iota((8, 256), 1) & 7)).astype(BF16)
    target = lax.dot_general(target_ref[...], tile, TN, preferred_element_type=F32)
    r, c = iota((256, 256), 0), iota((256, 256), 1)
    for side in range(2):
        total = low = 0.0
        for ref in sides[side]:
            total = total + ref[0:56].astype(F32)
            low = low + ref[56:58].astype(F32)
        total = total.reshape(448, 256) - target
        low = low[0] + low[1]
        low = low[0:4] + low[4:8]
        low = jnp.concatenate([low, low], axis=0)
        low = jnp.broadcast_to(low[None], (32, 8, 256)).reshape(256, 256)
        at = core if side == 0 else 1 - core
        low = jnp.where(((r >> 3) == (c >> 3)) & (((r & 7) >> 2) == at), low, 0.0)
        for _ in range(3):
            piece = low.astype(BF16)
            total = total + lax.dot_general(right, piece, TN, preferred_element_type=F32)
            low = low - piece.astype(F32)
        err_ref[at] = jnp.sum((total * total).reshape(56, 8, 256), axis=0)


def final_kernel(where_ref, err_ref, left_ref, own_ref, other_ref, query_ref, out_ref, fit_ref):
    core, chip = where_ref[0], where_ref[1]
    err = jnp.sum(err_ref[...], axis=0)
    at = iota((256, 512), 1)
    row = iota((256, 512), 0)
    member = ((at & 255) >> 3) * 2 + (at >> 8)
    err = jnp.where(member == (row >> 2), jnp.broadcast_to(err, (256, 512)), 0.0)
    fit = -(jnp.sum(err, axis=1, keepdims=True) / (256 * D))
    mean = jnp.sum(fit, axis=0, keepdims=True) / 256
    away = fit - mean
    spread = jnp.sum(away * away, axis=0, keepdims=True) / 256
    weight = away / jnp.sqrt(spread + spread_floor)
    me = iota((256, 128), 0) == 4 * (2 * chip + core)
    fit_ref[...] = jnp.sum(jnp.where(me, jnp.broadcast_to(fit, (256, 128)), 0.0), axis=0, keepdims=True)
    left = left_ref[...].astype(F32).reshape(256, 128) * weight
    turned = pltpu.roll(left.reshape(32, 8, 128), 4, 1)
    left = left.reshape(32, 8, 128)
    upper = iota((32, 8, 128), 1) < 4
    low = jnp.where(core == 0, left, turned)
    high = jnp.where(core == 0, turned, left)
    sums = [[0.0, 0.0], [0.0, 0.0]]
    for ref, first, second in ((own_ref, low, high), (other_ref, high, low)):
        for half, l in enumerate((jnp.where(upper, first, 0.0), jnp.where(upper, 0.0, second))):
            l = l.reshape(256, 128)
            parts = []
            for _ in range(3):
                parts.append(l.astype(BF16))
                l = l - parts[-1].astype(F32)
            l = jnp.concatenate(parts, axis=1)
            for which in range(2):
                right = ref[:, :, which * 512 : which * 512 + 512].astype(F32).reshape(256, 512).astype(BF16)
                g = lax.dot_general(l, right, TN, preferred_element_type=F32)
                a = 64 * which
                sums[which][half] += g[a : a + 56] + g[128 + a : 184 + a] + g[256 + a : 312 + a]
    for ref, (a, b) in zip((query_ref, out_ref), sums):
        ref[:, 0:512] = a
        ref[:, 512:896] = b[:, :384]


def call(kernel, out, args, name, smem=0, flops=10**9, scratch=()):
    return pl.pallas_call(
        kernel,
        out_shape=out,
        in_specs=[pl.BlockSpec(memory_space=pltpu.SMEM)] * smem + vmem(len(args) - smem),
        out_specs=jax.tree.map(lambda _: pl.BlockSpec(memory_space=pltpu.VMEM), out),
        scratch_shapes=scratch,
        name=name,
        cost_estimate=pl.CostEstimate(flops=flops, bytes_accessed=2 * 10**6, transcendentals=0),
        compiler_params=pltpu.CompilerParams(vmem_limit_bytes=40 * 2**20),
    )(*args)


def shape(s, t=BF16):
    return jax.ShapeDtypeStruct(s, t)


def after(x, y):
    return lax.optimization_barrier((x, y))[0]


def ints(*values):
    return jnp.stack([jnp.asarray(v, jnp.int32) for v in values])


SPLIT = 16


def per_device(
    tokens,
    target,
    w_query,
    w_key,
    w_value,
    w_out,
    query_left_factors,
    query_right_factors,
    o_left,
    o_right,
    member_ids,
):
    tok = tokens.shape[0]
    feats = w_query.shape[1]
    heads = feats // HEAD_DIM
    x, z, c = (lax.axis_index(a) for a in POP)
    y = lax.axis_index("mp")
    k = x * 8 + z
    p = 2 * k + c
    odd = member_ids[0] % 2
    half = jnp.where(odd == 0, 0.5, -0.5).astype(BF16)
    twice = jnp.where(odd == 0, 2.0, -2.0).astype(BF16)

    w_t = w_out.T
    first, second = w_t[:SPLIT], w_t[SPLIT:]
    along_x = lambda a: [a] + [shift(a, "pop_0", 4, d) for d in (1, 2, 3)]
    by_x = jnp.stack(along_x(first))
    z1, z7 = shift(second, "pop_1", 8, 1), shift(second, "pop_1", 8, 7)
    z2, z6 = shift(second, "pop_1", 8, 2), shift(second, "pop_1", 8, 6)
    z3, z5 = shift(z1, "pop_1", 8, 2), shift(z7, "pop_1", 8, 6)
    z4 = jnp.concatenate([shift(z2[:24], "pop_1", 8, 2), shift(z6[24:], "pop_1", 8, 6)], axis=0)
    by_z = jnp.stack([second, z1, z2, z3, z4, z5, z6, z7])
    seconds = along_x(by_z)
    up1, dn1 = shift(by_x, "pop_1", 8, 1), shift(by_x, "pop_1", 8, 7)
    up2, dn2 = shift(up1, "pop_1", 8, 1), shift(dn1, "pop_1", 8, 7)
    up3, dn3 = shift(up2, "pop_1", 8, 1), shift(dn2, "pop_1", 8, 7)
    up4 = jnp.concatenate([shift(up3[:2], "pop_1", 8, 1), shift(dn3[2:], "pop_1", 8, 7)], axis=0)
    firsts = [by_x, up1, up2, up3, up4, dn3, dn2, dn1]
    where = ints(*[((x - d) % 4 - y) % 4 for d in range(4)], *[(z - e) % 8 for e in range(8)])

    left_t = query_left_factors[0].T
    sent = call(
        front_kernel,
        shape((32, 8, 2048)),
        (
            ints(p, odd),
            tokens,
            w_query,
            jnp.pad(left_t, ((0, 124), (0, 0))),
            query_right_factors[0],
            o_left[0].T,
        ),
        "front",
        smem=1,
        scratch=[pltpu.VMEM((256, feats), F32)],
    )
    recv = lax.all_to_all(sent, CHIPS, 0, 0, tiled=True)

    cos_all, sin_all = tables(jnp.arange(tok, dtype=F32), HEAD_DIM)
    k32 = jnp.dot(tokens, w_key, preferred_element_type=F32)
    keys = (k32 * cos_all + jnp.roll(k32, 64, axis=1) * sin_all).astype(BF16)
    values = jnp.dot(tokens, w_value, preferred_element_type=F32).astype(BF16)
    cos8, sin8 = tables((k * 8).astype(F32) + jnp.arange(8, dtype=F32), HEAD_DIM)

    half_base = jnp.sum(recv[:, :, :feats].astype(F32), axis=0)
    mixed, low = call(
        functools.partial(attention_kernel, heads),
        (shape((256, feats)), shape((2, 8, 256), F32)),
        (ints(k * 8), recv, half_base, swap(half_base), keys, values, cos8, sin8),
        "attention",
        smem=1,
    )

    def project(mixed, low, name):
        return call(
            functools.partial(project_kernel, SPLIT),
            [shape((58, 8, 256))] * 4,
            (where, *firsts, *seconds, mixed, low),
            name,
            smem=1,
            scratch=[pltpu.VMEM((4, 56, 8, 256), BF16)],
        )

    def meet(outs):
        return [outs[0]] + [shift(outs[s], "mp", 4, s) for s in (1, 2, 3)]

    met = meet(project(mixed, low, "project_own"))
    met_b = meet(project(swap(mixed), swap(low), "project_other"))

    o_r = after(o_right[0], mixed)
    o_cut = lax.dynamic_slice(o_r, (0, feats * y), (RANK, feats)).reshape(RANK, 8, 2, 56)
    o_cut = jnp.moveaxis(o_cut, 2, 0).reshape(2, RANK, 448) * half
    o_cut = jnp.broadcast_to(o_cut[None], (32, 2, RANK, 448)).reshape(64, RANK, 448)
    cut_q = jnp.moveaxis((after(left_t, mixed) * twice).reshape(RANK, 64, 56), 1, 0)
    cut_o = jnp.moveaxis((o_r * twice).reshape(RANK, 64, 56), 1, 0)
    gap = jnp.zeros((64, RANK, 8), BF16)
    late = jnp.concatenate([cut_q, gap, cut_o, gap, o_cut, jnp.zeros((64, RANK, 64), BF16)], axis=2)
    late = lax.all_to_all(late, POP, 0, 0, tiled=True)
    factors = after(recv, mixed)[:, :, 1024:2048]
    factors_b = swap(factors)
    lefts = late[:, :, :128].reshape(32, 8, 128)
    right = late[:, :, 128:576].reshape(256, 448)

    goal = lax.dynamic_slice(target, (8 * k, 0), (8, feats)).reshape(8, 8, 2, 56)
    goal = jnp.where(c == 0, goal[:, :, 0], goal[:, :, 1]).reshape(8, 448)
    err = call(
        error_kernel,
        shape((2, 8, 256), F32),
        (ints(c), *met, *met_b, right, goal),
        "error",
        smem=1,
    )
    err = jnp.sum(err, axis=1).reshape(1, 1, 512)
    err = lax.all_to_all(jnp.broadcast_to(err, (16, 1, 512)), ("pop_0", "mp"), 0, 0, tiled=True)
    err = jnp.sum(err, axis=0, keepdims=True)
    err = lax.all_to_all(jnp.broadcast_to(err, (16, 1, 512)), ("pop_1", "pop_2"), 0, 0, tiled=True)
    grad_query, grad_out, fitness = call(
        final_kernel,
        [shape((56, feats), F32), shape((56, feats), F32), shape((1, 128), F32)],
        (ints(c, k), err, lefts, factors, factors_b),
        "final",
        smem=1,
    )
    return (grad_query, grad_out.T, fitness[0, :1])


def solution(mesh):
    torus = Mesh(mesh.devices.reshape(4, 8, 2, mesh.shape["mp"]), ("pop_0", "pop_1", "pop_2", "mp"))
    placed = (
        P(),
        P(None, "mp"),
        P(POP, "mp"),
        P(None, "mp"),
        P(None, "mp"),
        P("mp", POP),
        P(POP, None, None),
        P(POP, None, "mp"),
        P(POP, "mp", None),
        P(POP, None, None),
        P(POP),
    )
    return jax.shard_map(
        per_device,
        mesh=torus,
        in_specs=placed,
        out_specs=(P(POP, "mp"), P("mp", POP), P(POP)),
        check_vma=False,
    )
```

time: 174 us -> 182 us (1.046)
  waiting for transfers between devices: 68 us -> 40.1 us
  starting transfers between devices: 46.7 us -> 72.8 us
  blocking collectives: 0 us -> 13.4 us
  other arithmetic: 13.1 us -> 3.21 us
  Pallas kernels: 9.72 us -> 19.5 us
  matrix products: 7.36 us -> 1.25 us
  local copies, waits for them, and re-layouts: 23.7 us -> 28.5 us
    ppermute x11 -> x28, starting transfers between devices: 16.5 us -> 41.4 us  [shift(): return lax.ppermute(x, axis, [(i, (i + step) % size) for i in range(size)])]
    all_to_all x3 -> x2, waiting for transfers between devices: 27.7 us -> 6.44 us  [the longest x1 6.44 us: per_device(): lax.all_to_all(jnp.broadcast_to(err, (16, 1, 512)), ('pop_1', 'pop_2'), 0...]
    all_to_all x0 -> x1, blocking collectives: none -> 13.4 us  [per_device(): lax.all_to_all(jnp.broadcast_to(err, (16, 1, 512)), ('pop_0', 'mp'), 0, 0...]
    pallas_call x3 -> x6, Pallas kernels: 9.72 us -> 19.5 us  [call(): pl.pallas_call(kernel, out_shape=out, in_specs=[pl.BlockSpec(memory_space...]
    unnamed x31 -> x58, local copies, waits for them, and re-layouts: 7.71 us -> 14.3 us
    ppermute x11 -> x28, waiting for transfers between devices: 38 us -> 32.8 us  [shift(): return lax.ppermute(x, axis, [(i, (i + step) % size) for i in range(size)])]
    ppermute x6 -> x4, starting transfers between devices: 5.37 us -> 10.5 us  [swap(): return lax.ppermute(x, 'pop_2', [(0, 1), (1, 0)])]
    dot_general x4 -> x0, matrix products: 3.76 us -> none  [the longest x1 1.31 us: per_device(): jnp.dot(tokens, query_left_factors[0], preferred_element_type=F32)]
  transfers between devices with their start and end apart: 21 -> 35, of which waited for: 8 -> 9; matrix products, arithmetic and copies ran while one was open for 21% -> 10% of each run, Pallas kernels for 3% -> 9%
where the time goes in v2:
time: 182 us; the launch traced here: 181 us
  starting transfers between devices  72.8 us (40%)
  waiting for transfers between devices  40.1 us (22%)
  local copies, waits for them, and re-layouts  28.5 us (16%)
  Pallas kernels  19.5 us (11%)
  blocking collectives  13.4 us (7%)
  other arithmetic  3.21 us (2%)
  between operations  2.03 us (1%)
    ppermute x28, starting transfers between devices, shift(): return lax.ppermute(x, axis, [(i, (i + step) % size) for i in range(size)])  41.4 us
    ppermute x28, waiting for transfers between devices, shift(): return lax.ppermute(x, axis, [(i, (i + step) % size) for i in range(size)])  32.8 us
    pallas_call x6, Pallas kernels, call(): pl.pallas_call(kernel, out_shape=out, in_specs=[pl.BlockSpec(memory_space...  19.5 us
    unnamed x58, local copies, waits for them, and re-layouts  14.3 us
    all_to_all x1, blocking collectives, per_device(): lax.all_to_all(jnp.broadcast_to(err, (16, 1, 512)), ('pop_0', 'mp'), 0, 0...  13.4 us
    ppermute x4, starting transfers between devices, swap(): return lax.ppermute(x, 'pop_2', [(0, 1), (1, 0)])  10.5 us
    all_to_all x1, starting transfers between devices, per_device(): lax.all_to_all(jnp.broadcast_to(err, (16, 1, 512)), ('pop_1', 'pop_2'), 0...  8.63 us
    all_to_all x1, starting transfers between devices, per_device(): late = lax.all_to_all(late, POP, 0, 0, tiled=True)  6.69 us
  transfers between devices with their start and end apart: 35, of which 9 were waited for; matrix products, arithmetic and copies ran while one was open for 10% of the time, Pallas kernels for 9%

profile of v2, /device:TPU:1, one launch (start us, length us, event | category | flops | bytes accessed | tf_op | source)
XLA Modules:
  0.0 180.8 jit_solution(13454581294376506174)
XLA Ops:
  0.6 1.5 slice_bitcast_fusion
  2.1 3.6 %collective-permute-start.1 = (bf16[16,896]{1,0:T(8,128)(2,1)}, bf16[16,896]{1,0:T(8,128)(2,1)}, u32[]{:S(2)}, u32[]{:S(2)}) collective-permute-start(bf16[16,896]{1,0:T(8,128)(2,1)} %get-tuple-element.38), channel_id=1, source_target_pairs={{0,128},{64,192},{128,0},{192,64},{1,129},{65,193},{129,1},{193,65... | collective-permute-start | bytes 86024 | tf_op jit(solution)/shard_map/ppermute | solution.py:39
  6.0 2.4 %collective-permute-start.2 = (bf16[16,896]{1,0:T(8,128)(2,1)}, bf16[16,896]{1,0:T(8,128)(2,1)}, u32[]{:S(2)}, u32[]{:S(2)}) collective-permute-start(bf16[16,896]{1,0:T(8,128)(2,1)} %get-tuple-element.38), channel_id=1, source_target_pairs={{0,192},{64,0},{128,64},{192,128},{1,193},{65,1},{129,65},{193,129... | collective-permute-start | bytes 86024 | tf_op jit(solution)/shard_map/ppermute | solution.py:39
  8.3 1.5 slice.65
  9.9 6.0 %collective-permute-start.15 = (bf16[40,896]{1,0:T(8,128)(2,1)}, bf16[40,896]{1,0:T(8,128)(2,1)}, u32[]{:S(2)}, u32[]{:S(2)}) collective-permute-start(bf16[40,896]{1,0:T(8,128)(2,1)} %slice.65), channel_id=1, source_target_pairs={{0,48},{8,56},{16,0},{24,8},{32,16},{40,24},{48,32},{56,40},{1,49}... | collective-permute-start | bytes 215048 | tf_op jit(solution)/shard_map/ppermute | solution.py:39
  17.5 1.5 copy-done.1
  21.2 1.4 front.1
  22.6 1.0 copy-done.3
  23.6 5.5 %all-to-all-start = ((bf16[32,8,2048]{2,1,0:T(8,128)(2,1)}), bf16[32,8,2048]{2,1,0:T(8,128)(2,1)}, u32[]{:S(2)}, u32[]{:S(2)}) async-start(bf16[32,8,2048]{2,1,0:T(8,128)(2,1)} %copy-done.3), calls=%async_computation | async-start | bytes 2097152 | tf_op jit(solution)/shard_map/all_to_all | solution.py:297
  31.8 1.2 collective-permute-start.11
  33.1 1.5 collective-permute-start.17
  35.4 1.2 collective-permute-start.7
  37.7 16.2 %collective-permute-done.11 = bf16[40,896]{1,0:T(8,128)(2,1)S(1)} collective-permute-done((bf16[40,896]{1,0:T(8,128)(2,1)}, bf16[40,896]{1,0:T(8,128)(2,1)S(1)}, u32[]{:S(2)}, u32[]{:S(2)}) %collective-permute-start.11) | collective-permute-done | bytes 71712 | tf_op jit(solution)/shard_map/ppermute | solution.py:39
  53.9 1.9 %collective-permute-start.16 = (bf16[16,896]{1,0:T(8,128)(2,1)S(1)}, bf16[16,896]{1,0:T(8,128)(2,1)S(1)}, u32[]{:S(2)}, u32[]{:S(2)}) collective-permute-start(bf16[16,896]{1,0:T(8,128)(2,1)S(1)} %slice.67), channel_id=1, source_target_pairs={{0,48},{8,56},{16,0},{24,8},{32,16},{40,24},{48,32},{56,40},{1,49}... | collective-permute-start | bytes 86024 | tf_op jit(solution)/shard_map/ppermute | solution.py:39
  56.4 3.1 %collective-permute-start.14 = (bf16[24,896]{1,0:T(8,128)(2,1)S(1)}, bf16[24,896]{1,0:T(8,128)(2,1)S(1)}, u32[]{:S(2)}, u32[]{:S(2)}) collective-permute-start(bf16[24,896]{1,0:T(8,128)(2,1)S(1)} %slice.66), channel_id=1, source_target_pairs={{0,16},{8,24},{16,32},{24,40},{32,48},{40,56},{48,0},{56,8},{1,17}... | collective-permute-start | bytes 129032 | tf_op jit(solution)/shard_map/ppermute | solution.py:39
  59.5 2.9 %collective-permute-done.13 = bf16[40,896]{1,0:T(8,128)(2,1)S(1)} collective-permute-done((bf16[40,896]{1,0:T(8,128)(2,1)S(1)}, bf16[40,896]{1,0:T(8,128)(2,1)S(1)}, u32[]{:S(2)}, u32[]{:S(2)}) %collective-permute-start.13) | collective-permute-done | bytes 71712 | tf_op jit(solution)/shard_map/ppermute | solution.py:39
  63.3 1.9 %collective-permute-start.8 = (bf16[4,16,896]{2,1,0:T(8,128)(2,1)S(1)}, bf16[4,16,896]{2,1,0:T(8,128)(2,1)S(1)}, u32[]{:S(2)}, u32[]{:S(2)}) collective-permute-start(bf16[4,16,896]{2,1,0:T(8,128)(2,1)S(1)} %collective-permute-done.7.refs_7_), channel_id=1, source_target_pairs={{0,56},{8,0},{16,8},{24,16},{32,24},{40,32},{48,40},{56,48},{1,57}... | collective-permute-start | bytes 344072 | tf_op jit(solution)/shard_map/ppermute | solution.py:39
  65.3 1.5 collective-permute-done.18
  66.8 0.9 bitcast_dynamic-update-slice_fusion.1
  68.0 2.1 %collective-permute-start.9 = (bf16[4,16,896]{2,1,0:T(8,128)(2,1)S(1)}, bf16[4,16,896]{2,1,0:T(8,128)(2,1)S(1)}, u32[]{:S(2)}, u32[]{:S(2)}) collective-permute-start(bf16[4,16,896]{2,1,0:T(8,128)(2,1)S(1)} %collective-permute-done.8.refs_6_), channel_id=1, source_target_pairs={{0,56},{8,0},{16,8},{24,16},{32,24},{40,32},{48,40},{56,48},{1,57}... | collective-permute-start | bytes 344072 | tf_op jit(solution)/shard_map/ppermute | solution.py:39
  70.1 2.6 %collective-permute-start.21 = (bf16[8,40,896]{2,1,0:T(8,128)(2,1)S(1)}, bf16[8,40,896]{2,1,0:T(8,128)(2,1)S(1)}, u32[]{:S(2)}, u32[]{:S(2)}) collective-permute-start(bf16[8,40,896]{2,1,0:T(8,128)(2,1)S(1)} %bitcast_dynamic-update-slice_fusion.refs_8_), channel_id=1, source_target_pairs={{0,192},{64,0},{128,64},{192,128},{1,193},{65,1},{129,65},{193,129... | collective-permute-start | bytes 1720328 | tf_op jit(solution)/shard_map/ppermute | solution.py:39
  74.6 2.7 %collective-permute-start.10 = (bf16[2,16,896]{2,1,0:T(8,128)(2,1)}, bf16[2,16,896]{2,1,0:T(8,128)(2,1)}, u32[]{:S(2)}, u32[]{:S(2)}) collective-permute-start(bf16[2,16,896]{2,1,0:T(8,128)(2,1)} %slice.64), channel_id=1, source_target_pairs={{0,56},{8,0},{16,8},{24,16},{32,24},{40,32},{48,40},{56,48},{1,57}... | collective-permute-start | bytes 172040 | tf_op jit(solution)/shard_map/ppermute | solution.py:39
  77.3 1.1 convert_reduce_fusion.base_ref
  78.4 3.6 %collective-permute-done.6 = bf16[2,16,896]{2,1,0:T(8,128)(2,1)S(1)} collective-permute-done((bf16[2,16,896]{2,1,0:T(8,128)(2,1)S(1)}, bf16[2,16,896]{2,1,0:T(8,128)(2,1)S(1)}, u32[]{:S(2)}, u32[]{:S(2)}) %collective-permute-start.6) | collective-permute-done | bytes 57376 | tf_op jit(solution)/shard_map/ppermute | solution.py:39
  82.1 8.8 %collective-permute-start.22 = (f32[8,896]{1,0:T(8,128)S(1)}, f32[8,896]{1,0:T(8,128)S(1)}, u32[]{:S(2)}, u32[]{:S(2)}) collective-permute-start(f32[8,896]{1,0:T(8,128)S(1)} %convert_reduce_fusion.base_ref), channel_id=1, source_target_pairs={{0,4},{4,0},{1,5},{5,1},{2,6},{6,2},{3,7},{7,3},{8,12},{12,8},{9,1... | collective-permute-start | bytes 86024 | tf_op jit(solution)/shard_map/ppermute | solution.py:43
  91.8 5.0 %attention.1 = (bf16[256,896]{1,0:T(8,128)(2,1)}, f32[2,8,256]{2,1,0:T(8,128)S(1)}) custom-call(s32[1]{0:T(128)} %bitcast.27.first_ref, bf16[32,8,2048]{2,1,0:T(8,128)(2,1)} %all-to-all-done.recv_ref, f32[8,896]{1,0:T(8,128)S(1)} %convert_reduce_fusion.base_ref, f32[8,896]{1,0:T(8,128)S(1)} %collective-permute-done.22.other_ref, ...), custom_call_target="tpu_custom_call" | custom-call | flops 1000000000 | bytes 2000000 | tf_op jit(solution)/shard_map/attention/pallas_call | solution.py:213
  98.6 2.0 %concatenate.32 = bf16[64,4,640]{2,1,0:T(4,128)(2,1)} concatenate(bf16[64,4,56]{2,1,0:T(4,128)(2,1)S(1)} %copy.41, bf16[64,4,8]{2,1,0:T(4,128)(2,1)S(1)} %broadcast_in_dim.12, bf16[64,4,56]{2,1,0:T(4,128)(2,1)S(1)} %copy.42, bf16[64,4,8]{2,1,0:T(4,128)(2,1)S(1)} %broadcast_in_dim.12, bf16[64,4,448]{2,1,0:T(4,128)(2,1)S(1)} %bitcast.74, bf16[64,4,64]{2,1,0:T(4,128)(2,1)} %broadcast_in_dim.14), dimensions={2} | concatenate | bytes 655360 | tf_op jit(solution)/shard_map/concatenate | solution.py:337
  100.6 6.7 %all-to-all-start.1 = ((bf16[64,4,640]{2,1,0:T(4,128)(2,1)}), bf16[64,4,640]{2,1,0:T(4,128)(2,1)}, u32[]{:S(2)}, u32[]{:S(2)}) async-start(bf16[64,4,640]{2,1,0:T(4,128)(2,1)} %concatenate.32), calls=%async_computation.1 | async-start | bytes 655360 | tf_op jit(solution)/shard_map/all_to_all | solution.py:338
  108.2 4.2 %project_own.1 = (bf16[58,8,256]{2,1,0:T(8,128)(2,1)S(1)}, bf16[58,8,256]{2,1,0:T(8,128)(2,1)S(1)}, bf16[58,8,256]{2,1,0:T(8,128)(2,1)S(1)}, bf16[58,8,256]{2,1,0:T(8,128)(2,1)}) custom-call(s32[12]{0:T(128)S(1)} %stack.118.where_ref, bf16[4,16,896]{2,1,0:T(8,128)(2,1)S(1)} %pad_maximum_fusion.refs_0_, ...), custom_call_target="tpu_custom_call" | custom-call | flops 1000000000 | bytes 2000000 | tf_op jit(solution)/shard_map/project_own/pallas_call | solution.py:213
  113.1 1.3 collective-permute-start.23
  114.4 2.6 %collective-permute-start.24 = (bf16[58,8,256]{2,1,0:T(8,128)(2,1)S(1)}, bf16[58,8,256]{2,1,0:T(8,128)(2,1)S(1)}, u32[]{:S(2)}, u32[]{:S(2)}) collective-permute-start(bf16[58,8,256]{2,1,0:T(8,128)(2,1)S(1)} %get-tuple-element.23), channel_id=1, source_target_pairs={{0,2},{1,3},{2,0},{3,1},{4,6},{5,7},{6,4},{7,5},{8,10},{9,11},{10,... | collective-permute-start | bytes 712712 | tf_op jit(solution)/shard_map/ppermute | solution.py:39
  117.0 1.1 collective-permute-start.27
  118.1 1.1 slice.60.own_ref
  119.1 1.1 collective-permute-start.25
  120.6 0.9 copy-done.10
  122.4 0.9 copy-done.14
  124.2 4.2 %project_other.1 = (bf16[58,8,256]{2,1,0:T(8,128)(2,1)S(1)}, bf16[58,8,256]{2,1,0:T(8,128)(2,1)}, bf16[58,8,256]{2,1,0:T(8,128)(2,1)}, bf16[58,8,256]{2,1,0:T(8,128)(2,1)}) custom-call(s32[12]{0:T(128)S(1)} %stack.118.where_ref, bf16[4,16,896]{2,1,0:T(8,128)(2,1)S(1)} %pad_maximum_fusion.refs_0_, bf16[4,16,896]{2,1,0:T(8,128)(2,1)S(1)} %copy-done.12, ...), custom_call_target="tpu_custom_call" | custom-call | flops 1000000000 | bytes 2000000 | tf_op jit(solution)/shard_map/project_other/pallas_call | solution.py:213
  130.9 1.8 collective-permute-start.30
  133.7 1.0 slice.71
  134.9 7.9 %collective-permute-done.28.refs_5_ = bf16[58,8,256]{2,1,0:T(8,128)(2,1)S(1)} collective-permute-done((bf16[58,8,256]{2,1,0:T(8,128)(2,1)}, bf16[58,8,256]{2,1,0:T(8,128)(2,1)S(1)}, u32[]{:S(2)}, u32[]{:S(2)}) %collective-permute-start.28) | collective-permute-done | bytes 237600 | tf_op jit(solution)/shard_map/ppermute | solution.py:39
  143.1 0.9 copy-done.8
  144.0 0.9 copy-done.18
  145.0 0.9 copy-done.20
  145.9 1.7 error.1
  147.6 13.4 %all_to_all.20 = f32[16,1,512]{2,1,0:T(1,128)S(1)} all-to-all(f32[16,1,512]{2,1,0:T(1,128)S(1)} %broadcast_in_dim.16), channel_id=1, replica_groups=mesh['pop_0'=4,'pop_1'=8,'pop_2'=2,'mp'=4] {'pop_0','mp'}, dimensions={0} | all-to-all | bytes 65536 | tf_op jit(solution)/shard_map/all_to_all | solution.py:354
  161.8 8.6 %all-to-all-start.3 = ((f32[16,1,512]{2,1,0:T(1,128)}), f32[16,1,512]{2,1,0:T(1,128)S(1)}, u32[]{:S(2)}, u32[]{:S(2)}) async-start(f32[16,1,512]{2,1,0:T(1,128)} %broadcast_in_dim.34), calls=%async_computation.3 | async-start | bytes 65536 | tf_op jit(solution)/shard_map/all_to_all | solution.py:356
  171.4 6.4 %all-to-all-done.3.err_ref = f32[16,1,512]{2,1,0:T(1,128)S(1)} async-done(((f32[16,1,512]{2,1,0:T(1,128)}), f32[16,1,512]{2,1,0:T(1,128)S(1)}, u32[]{:S(2)}, u32[]{:S(2)}) %all-to-all-start.3) | async-done | bytes 32800 | tf_op jit(solution)/shard_map/all_to_all | solution.py:356
  177.8 3.0 %final.1 = (f32[56,896]{1,0:T(8,128)}, f32[56,896]{1,0:T(8,128)}, f32[1,128]{1,0:T(1,128)}) custom-call(s32[2]{0:T(128)S(1)} %pad_add_fusion.where_ref, f32[16,1,512]{2,1,0:T(1,128)S(1)} %all-to-all-done.3.err_ref, bf16[32,8,128]{2,1,0:T(8,128)(2,1)S(1)} %bitcast.71, bf16[32,8,1024]{2,1,0:T(8,128)(2,1)S(1)} %slice.60.own_ref, ...), custom_call_target="tpu_custom_call" | custom-call | flops 1000000000 | bytes 2000000 | tf_op jit(solution)/shard_map/final/pallas_call | solution.py:213
  (137 shorter events, 23.4 us)
Async XLA Ops:
  0.6 28.6 %copy-start = (bf16[3584,128]{1,0:T(8,128)(2,1)S(1)}, bf16[3584,128]{1,0:T(8,128)(2,1)}, u32[]{:S(2)}) copy-start(bf16[3584,128]{1,0:T(8,128)(2,1)} %param.14) | copy-start | bytes 2752516
  2.1 29.7 %collective-permute-start.1 = (bf16[16,896]{1,0:T(8,128)(2,1)}, bf16[16,896]{1,0:T(8,128)(2,1)}, u32[]{:S(2)}, u32[]{:S(2)}) collective-permute-start(bf16[16,896]{1,0:T(8,128)(2,1)} %get-tuple-element.38), channel_id=1, source_target_pairs={{0,128},{64,192},{128,0},{192,64},{1,129},{65,193},{129,1},{193,65... | collective-permute-start | bytes 86024 | tf_op jit(solution)/shard_map/ppermute | solution.py:39
  5.7 27.4 %collective-permute-start = (bf16[16,896]{1,0:T(8,128)(2,1)}, bf16[16,896]{1,0:T(8,128)(2,1)}, u32[]{:S(2)}, u32[]{:S(2)}) collective-permute-start(bf16[16,896]{1,0:T(8,128)(2,1)} %get-tuple-element.38), channel_id=1, source_target_pairs={{0,64},{64,128},{128,192},{192,0},{1,65},{65,129},{129,193},{193,1... | collective-permute-start | bytes 86024 | tf_op jit(solution)/shard_map/ppermute | solution.py:39
  6.0 28.6 %collective-permute-start.2 = (bf16[16,896]{1,0:T(8,128)(2,1)}, bf16[16,896]{1,0:T(8,128)(2,1)}, u32[]{:S(2)}, u32[]{:S(2)}) collective-permute-start(bf16[16,896]{1,0:T(8,128)(2,1)} %get-tuple-element.38), channel_id=1, source_target_pairs={{0,192},{64,0},{128,64},{192,128},{1,193},{65,1},{129,65},{193,129... | collective-permute-start | bytes 86024 | tf_op jit(solution)/shard_map/ppermute | solution.py:39
  9.9 26.8 %collective-permute-start.15 = (bf16[40,896]{1,0:T(8,128)(2,1)}, bf16[40,896]{1,0:T(8,128)(2,1)}, u32[]{:S(2)}, u32[]{:S(2)}) collective-permute-start(bf16[40,896]{1,0:T(8,128)(2,1)} %slice.65), channel_id=1, source_target_pairs={{0,48},{8,56},{16,0},{24,8},{32,16},{40,24},{48,32},{56,40},{1,49}... | collective-permute-start | bytes 215048 | tf_op jit(solution)/shard_map/ppermute | solution.py:39
  15.9 39.9 %collective-permute-start.12 = (bf16[40,896]{1,0:T(8,128)(2,1)}, bf16[40,896]{1,0:T(8,128)(2,1)S(1)}, u32[]{:S(2)}, u32[]{:S(2)}) collective-permute-start(bf16[40,896]{1,0:T(8,128)(2,1)} %slice.65), channel_id=1, source_target_pairs={{0,16},{8,24},{16,32},{24,40},{32,48},{40,56},{48,0},{56,8},{1,17}... | collective-permute-start | bytes 215048 | tf_op jit(solution)/shard_map/ppermute | solution.py:39
  17.4 1.5 copy-start.1
  22.6 1.0 copy-start.3
  23.6 5.5 %copy-start.22 = (bf16[896,56]{0,1:T(8,128)(2,1)S(1)}, bf16[896,56]{0,1:T(8,128)(2,1)}, u32[]{:S(2)}) copy-start(bf16[896,56]{0,1:T(8,128)(2,1)} %param.16) | copy-start | bytes 301060
  23.6 5.6 %copy-start.2 = (bf16[256,3584]{1,0:T(8,128)(2,1)S(1)}, bf16[256,3584]{1,0:T(8,128)(2,1)}, u32[]{:S(2)}) copy-start(bf16[256,3584]{1,0:T(8,128)(2,1)} %tokens_ref.1) | copy-start | bytes 5505028
  23.6 53.7 %all-to-all-start = ((bf16[32,8,2048]{2,1,0:T(8,128)(2,1)}), bf16[32,8,2048]{2,1,0:T(8,128)(2,1)}, u32[]{:S(2)}, u32[]{:S(2)}) async-start(bf16[32,8,2048]{2,1,0:T(8,128)(2,1)} %copy-done.3), calls=%async_computation | async-start | bytes 2097152 | tf_op jit(solution)/shard_map/all_to_all | solution.py:297
  29.2 1.5 copy-start.21
  31.8 22.1 %collective-permute-start.11 = (bf16[40,896]{1,0:T(8,128)(2,1)}, bf16[40,896]{1,0:T(8,128)(2,1)S(1)}, u32[]{:S(2)}, u32[]{:S(2)}) collective-permute-start(bf16[40,896]{1,0:T(8,128)(2,1)} %slice.65), channel_id=1, source_target_pairs={{0,8},{8,16},{16,24},{24,32},{32,40},{40,48},{48,56},{56,0},{1,9},... | collective-permute-start | bytes 215048 | tf_op jit(solution)/shard_map/ppermute | solution.py:39
  33.1 23.3 %collective-permute-start.17 = (bf16[40,896]{1,0:T(8,128)(2,1)}, bf16[40,896]{1,0:T(8,128)(2,1)S(1)}, u32[]{:S(2)}, u32[]{:S(2)}) collective-permute-start(bf16[40,896]{1,0:T(8,128)(2,1)} %slice.65), channel_id=1, source_target_pairs={{0,56},{8,0},{16,8},{24,16},{32,24},{40,32},{48,40},{56,48},{1,57}... | collective-permute-start | bytes 215048 | tf_op jit(solution)/shard_map/ppermute | solution.py:39
  35.4 27.9 %collective-permute-start.7 = (bf16[4,16,896]{2,1,0:T(8,128)(2,1)S(1)}, bf16[4,16,896]{2,1,0:T(8,128)(2,1)S(1)}, u32[]{:S(2)}, u32[]{:S(2)}) collective-permute-start(bf16[4,16,896]{2,1,0:T(8,128)(2,1)S(1)} %pad_maximum_fusion.refs_0_), channel_id=1, source_target_pairs={{0,56},{8,0},{16,8},{24,16},{32,24},{40,32},{48,40},{56,48},{1,57}... | collective-permute-start | bytes 344072 | tf_op jit(solution)/shard_map/ppermute | solution.py:39
  36.6 28.6 %collective-permute-start.3 = (bf16[4,16,896]{2,1,0:T(8,128)(2,1)S(1)}, bf16[4,16,896]{2,1,0:T(8,128)(2,1)S(1)}, u32[]{:S(2)}, u32[]{:S(2)}) collective-permute-start(bf16[4,16,896]{2,1,0:T(8,128)(2,1)S(1)} %pad_maximum_fusion.refs_0_), channel_id=1, source_target_pairs={{0,8},{8,16},{16,24},{24,32},{32,40},{40,48},{48,56},{56,0},{1,9},... | collective-permute-start | bytes 344072 | tf_op jit(solution)/shard_map/ppermute | solution.py:39
  53.9 11.4 %collective-permute-start.16 = (bf16[16,896]{1,0:T(8,128)(2,1)S(1)}, bf16[16,896]{1,0:T(8,128)(2,1)S(1)}, u32[]{:S(2)}, u32[]{:S(2)}) collective-permute-start(bf16[16,896]{1,0:T(8,128)(2,1)S(1)} %slice.67), channel_id=1, source_target_pairs={{0,48},{8,56},{16,0},{24,8},{32,16},{40,24},{48,32},{56,40},{1,49}... | collective-permute-start | bytes 86024 | tf_op jit(solution)/shard_map/ppermute | solution.py:39
  55.8 6.6 %collective-permute-start.13 = (bf16[40,896]{1,0:T(8,128)(2,1)S(1)}, bf16[40,896]{1,0:T(8,128)(2,1)S(1)}, u32[]{:S(2)}, u32[]{:S(2)}) collective-permute-start(bf16[40,896]{1,0:T(8,128)(2,1)S(1)} %collective-permute-done.11), channel_id=1, source_target_pairs={{0,16},{8,24},{16,32},{24,40},{32,48},{40,56},{48,0},{56,8},{1,17}... | collective-permute-start | bytes 215048 | tf_op jit(solution)/shard_map/ppermute | solution.py:39
  56.4 8.9 %collective-permute-start.14 = (bf16[24,896]{1,0:T(8,128)(2,1)S(1)}, bf16[24,896]{1,0:T(8,128)(2,1)S(1)}, u32[]{:S(2)}, u32[]{:S(2)}) collective-permute-start(bf16[24,896]{1,0:T(8,128)(2,1)S(1)} %slice.66), channel_id=1, source_target_pairs={{0,16},{8,24},{16,32},{24,40},{32,48},{40,56},{48,0},{56,8},{1,17}... | collective-permute-start | bytes 129032 | tf_op jit(solution)/shard_map/ppermute | solution.py:39
  62.4 4.4 %collective-permute-start.18 = (bf16[40,896]{1,0:T(8,128)(2,1)S(1)}, bf16[40,896]{1,0:T(8,128)(2,1)S(1)}, u32[]{:S(2)}, u32[]{:S(2)}) collective-permute-start(bf16[40,896]{1,0:T(8,128)(2,1)S(1)} %collective-permute-done.17), channel_id=1, source_target_pairs={{0,48},{8,56},{16,0},{24,8},{32,16},{40,24},{48,32},{56,40},{1,49}... | collective-permute-start | bytes 215048 | tf_op jit(solution)/shard_map/ppermute | solution.py:39
  63.3 44.9 %copy-start.9 = (bf16[4,16,896]{2,1,0:T(8,128)(2,1)}, bf16[4,16,896]{2,1,0:T(8,128)(2,1)S(1)}, u32[]{:S(2)}) copy-start(bf16[4,16,896]{2,1,0:T(8,128)(2,1)S(1)} %collective-permute-done.7.refs_7_) | copy-start | bytes 344068
  63.3 4.7 %collective-permute-start.8 = (bf16[4,16,896]{2,1,0:T(8,128)(2,1)S(1)}, bf16[4,16,896]{2,1,0:T(8,128)(2,1)S(1)}, u32[]{:S(2)}, u32[]{:S(2)}) collective-permute-start(bf16[4,16,896]{2,1,0:T(8,128)(2,1)S(1)} %collective-permute-done.7.refs_7_), channel_id=1, source_target_pairs={{0,56},{8,0},{16,8},{24,16},{32,24},{40,32},{48,40},{56,48},{1,57}... | collective-permute-start | bytes 344072 | tf_op jit(solution)/shard_map/ppermute | solution.py:39
  65.2 43.0 %copy-start.11 = (bf16[4,16,896]{2,1,0:T(8,128)(2,1)}, bf16[4,16,896]{2,1,0:T(8,128)(2,1)S(1)}, u32[]{:S(2)}) copy-start(bf16[4,16,896]{2,1,0:T(8,128)(2,1)S(1)} %collective-permute-done.3.refs_1_) | copy-start | bytes 344068
  65.2 4.9 %collective-permute-start.4 = (bf16[4,16,896]{2,1,0:T(8,128)(2,1)S(1)}, bf16[4,16,896]{2,1,0:T(8,128)(2,1)S(1)}, u32[]{:S(2)}, u32[]{:S(2)}) collective-permute-start(bf16[4,16,896]{2,1,0:T(8,128)(2,1)S(1)} %collective-permute-done.3.refs_1_), channel_id=1, source_target_pairs={{0,8},{8,16},{16,24},{24,32},{32,40},{40,48},{48,56},{56,0},{1,9},... | collective-permute-start | bytes 344072 | tf_op jit(solution)/shard_map/ppermute | solution.py:39
  68.0 40.2 %copy-start.13 = (bf16[4,16,896]{2,1,0:T(8,128)(2,1)}, bf16[4,16,896]{2,1,0:T(8,128)(2,1)S(1)}, u32[]{:S(2)}) copy-start(bf16[4,16,896]{2,1,0:T(8,128)(2,1)S(1)} %collective-permute-done.8.refs_6_) | copy-start | bytes 344068
  68.0 5.9 %collective-permute-start.9 = (bf16[4,16,896]{2,1,0:T(8,128)(2,1)S(1)}, bf16[4,16,896]{2,1,0:T(8,128)(2,1)S(1)}, u32[]{:S(2)}, u32[]{:S(2)}) collective-permute-start(bf16[4,16,896]{2,1,0:T(8,128)(2,1)S(1)} %collective-permute-done.8.refs_6_), channel_id=1, source_target_pairs={{0,56},{8,0},{16,8},{24,16},{32,24},{40,32},{48,40},{56,48},{1,57}... | collective-permute-start | bytes 344072 | tf_op jit(solution)/shard_map/ppermute | solution.py:39
  70.1 38.1 %copy-start.15 = (bf16[4,16,896]{2,1,0:T(8,128)(2,1)}, bf16[4,16,896]{2,1,0:T(8,128)(2,1)S(1)}, u32[]{:S(2)}) copy-start(bf16[4,16,896]{2,1,0:T(8,128)(2,1)S(1)} %collective-permute-done.4.refs_2_) | copy-start | bytes 344068
  70.1 7.1 %collective-permute-start.5 = (bf16[4,16,896]{2,1,0:T(8,128)(2,1)S(1)}, bf16[4,16,896]{2,1,0:T(8,128)(2,1)S(1)}, u32[]{:S(2)}, u32[]{:S(2)}) collective-permute-start(bf16[4,16,896]{2,1,0:T(8,128)(2,1)S(1)} %collective-permute-done.4.refs_2_), channel_id=1, source_target_pairs={{0,8},{8,16},{16,24},{24,32},{32,40},{40,48},{48,56},{56,0},{1,9},... | collective-permute-start | bytes 344072 | tf_op jit(solution)/shard_map/ppermute | solution.py:39
  70.1 38.0 %collective-permute-start.21 = (bf16[8,40,896]{2,1,0:T(8,128)(2,1)S(1)}, bf16[8,40,896]{2,1,0:T(8,128)(2,1)S(1)}, u32[]{:S(2)}, u32[]{:S(2)}) collective-permute-start(bf16[8,40,896]{2,1,0:T(8,128)(2,1)S(1)} %bitcast_dynamic-update-slice_fusion.refs_8_), channel_id=1, source_target_pairs={{0,192},{64,0},{128,64},{192,128},{1,193},{65,1},{129,65},{193,129... | collective-permute-start | bytes 1720328 | tf_op jit(solution)/shard_map/ppermute | solution.py:39
  72.7 35.4 %collective-permute-start.20 = (bf16[8,40,896]{2,1,0:T(8,128)(2,1)S(1)}, bf16[8,40,896]{2,1,0:T(8,128)(2,1)}, u32[]{:S(2)}, u32[]{:S(2)}) collective-permute-start(bf16[8,40,896]{2,1,0:T(8,128)(2,1)S(1)} %bitcast_dynamic-update-slice_fusion.refs_8_), channel_id=1, source_target_pairs={{0,128},{64,192},{128,0},{192,64},{1,129},{65,193},{129,1},{193,65... | collective-permute-start | bytes 1720328 | tf_op jit(solution)/shard_map/ppermute | solution.py:39
  73.4 34.8 %collective-permute-start.19 = (bf16[8,40,896]{2,1,0:T(8,128)(2,1)S(1)}, bf16[8,40,896]{2,1,0:T(8,128)(2,1)}, u32[]{:S(2)}, u32[]{:S(2)}) collective-permute-start(bf16[8,40,896]{2,1,0:T(8,128)(2,1)S(1)} %bitcast_dynamic-update-slice_fusion.refs_8_), channel_id=1, source_target_pairs={{0,64},{64,128},{128,192},{192,0},{1,65},{65,129},{129,193},{193,1... | collective-permute-start | bytes 1720328 | tf_op jit(solution)/shard_map/ppermute | solution.py:39
  74.6 32.7 %collective-permute-start.10 = (bf16[2,16,896]{2,1,0:T(8,128)(2,1)}, bf16[2,16,896]{2,1,0:T(8,128)(2,1)}, u32[]{:S(2)}, u32[]{:S(2)}) collective-permute-start(bf16[2,16,896]{2,1,0:T(8,128)(2,1)} %slice.64), channel_id=1, source_target_pairs={{0,56},{8,0},{16,8},{24,16},{32,24},{40,32},{48,40},{56,48},{1,57}... | collective-permute-start | bytes 172040 | tf_op jit(solution)/shard_map/ppermute | solution.py:39
  77.2 4.8 %collective-permute-start.6 = (bf16[2,16,896]{2,1,0:T(8,128)(2,1)S(1)}, bf16[2,16,896]{2,1,0:T(8,128)(2,1)S(1)}, u32[]{:S(2)}, u32[]{:S(2)}) collective-permute-start(bf16[2,16,896]{2,1,0:T(8,128)(2,1)S(1)} %slice.63), channel_id=1, source_target_pairs={{0,8},{8,16},{16,24},{24,32},{32,40},{40,48},{48,56},{56,0},{1,9},... | collective-permute-start | bytes 172040 | tf_op jit(solution)/shard_map/ppermute | solution.py:39
  82.1 9.7 %collective-permute-start.22 = (f32[8,896]{1,0:T(8,128)S(1)}, f32[8,896]{1,0:T(8,128)S(1)}, u32[]{:S(2)}, u32[]{:S(2)}) collective-permute-start(f32[8,896]{1,0:T(8,128)S(1)} %convert_reduce_fusion.base_ref), channel_id=1, source_target_pairs={{0,4},{4,0},{1,5},{5,1},{2,6},{6,2},{3,7},{7,3},{8,12},{12,8},{9,1... | collective-permute-start | bytes 86024 | tf_op jit(solution)/shard_map/ppermute | solution.py:43
  91.8 5.4 %copy-start.23 = (bf16[1,3584,4]{1,2,0:T(4,128)(2,1)S(1)}, bf16[1,3584,4]{1,2,0:T(4,128)(2,1)}, u32[]{:S(2)}) copy-start(bf16[1,3584,4]{1,2,0:T(4,128)(2,1)} %param.17) | copy-start | bytes 86020
  91.8 5.4 %copy-start.24 = (bf16[1,4,3584]{2,1,0:T(4,128)(2,1)S(1)}, bf16[1,4,3584]{2,1,0:T(4,128)(2,1)}, u32[]{:S(2)}) copy-start(bf16[1,4,3584]{2,1,0:T(4,128)(2,1)} %param.20) | copy-start | bytes 86020
  96.8 23.8 %collective-permute-start.26 = (bf16[256,896]{1,0:T(8,128)(2,1)}, bf16[256,896]{1,0:T(8,128)(2,1)}, u32[]{:S(2)}, u32[]{:S(2)}) collective-permute-start(bf16[256,896]{1,0:T(8,128)(2,1)} %get-tuple-element.19.refs_12_), channel_id=1, source_target_pairs={{0,4},{4,0},{1,5},{5,1},{2,6},{6,2},{3,7},{7,3},{8,12},{12,8},{9,1... | collective-permute-start | bytes 1376264 | tf_op jit(solution)/shard_map/ppermute | solution.py:43
  100.6 33.1 %all-to-all-start.1 = ((bf16[64,4,640]{2,1,0:T(4,128)(2,1)}), bf16[64,4,640]{2,1,0:T(4,128)(2,1)}, u32[]{:S(2)}, u32[]{:S(2)}) async-start(bf16[64,4,640]{2,1,0:T(4,128)(2,1)} %concatenate.32), calls=%async_computation.1 | async-start | bytes 655360 | tf_op jit(solution)/shard_map/all_to_all | solution.py:338
  113.1 16.4 %collective-permute-start.23 = (bf16[58,8,256]{2,1,0:T(8,128)(2,1)S(1)}, bf16[58,8,256]{2,1,0:T(8,128)(2,1)S(1)}, u32[]{:S(2)}, u32[]{:S(2)}) collective-permute-start(bf16[58,8,256]{2,1,0:T(8,128)(2,1)S(1)} %get-tuple-element.22), channel_id=1, source_target_pairs={{0,1},{1,2},{2,3},{3,0},{4,5},{5,6},{6,7},{7,4},{8,9},{9,10},{10,1... | collective-permute-start | bytes 712712 | tf_op jit(solution)/shard_map/ppermute | solution.py:39
  114.4 15.8 %collective-permute-start.24 = (bf16[58,8,256]{2,1,0:T(8,128)(2,1)S(1)}, bf16[58,8,256]{2,1,0:T(8,128)(2,1)S(1)}, u32[]{:S(2)}, u32[]{:S(2)}) collective-permute-start(bf16[58,8,256]{2,1,0:T(8,128)(2,1)S(1)} %get-tuple-element.23), channel_id=1, source_target_pairs={{0,2},{1,3},{2,0},{3,1},{4,6},{5,7},{6,4},{7,5},{8,10},{9,11},{10,... | collective-permute-start | bytes 712712 | tf_op jit(solution)/shard_map/ppermute | solution.py:39
  117.0 3.3 %collective-permute-start.27 = (f32[2,8,256]{2,1,0:T(8,128)S(1)}, f32[2,8,256]{2,1,0:T(8,128)S(1)}, u32[]{:S(2)}, u32[]{:S(2)}) collective-permute-start(f32[2,8,256]{2,1,0:T(8,128)S(1)} %get-tuple-element.20.refs_13_), channel_id=1, source_target_pairs={{0,4},{4,0},{1,5},{5,1},{2,6},{6,2},{3,7},{7,3},{8,12},{12,8},{9,1... | collective-permute-start | bytes 49160 | tf_op jit(solution)/shard_map/ppermute | solution.py:43
  119.1 15.7 %collective-permute-start.25 = (bf16[58,8,256]{2,1,0:T(8,128)(2,1)}, bf16[58,8,256]{2,1,0:T(8,128)(2,1)}, u32[]{:S(2)}, u32[]{:S(2)}) collective-permute-start(bf16[58,8,256]{2,1,0:T(8,128)(2,1)} %get-tuple-element.24), channel_id=1, source_target_pairs={{0,3},{1,0},{2,1},{3,2},{4,7},{5,4},{6,5},{7,6},{8,11},{9,8},{10,9... | collective-permute-start | bytes 712712 | tf_op jit(solution)/shard_map/ppermute | solution.py:39
  120.3 51.1 %collective-permute-start.31 = (bf16[32,8,1024]{2,1,0:T(8,128)(2,1)S(1)}, bf16[32,8,1024]{2,1,0:T(8,128)(2,1)}, u32[]{:S(2)}, u32[]{:S(2)}) collective-permute-start(bf16[32,8,1024]{2,1,0:T(8,128)(2,1)S(1)} %slice.60.own_ref), channel_id=1, source_target_pairs={{0,4},{4,0},{1,5},{5,1},{2,6},{6,2},{3,7},{7,3},{8,12},{12,8},{9,1... | collective-permute-start | bytes 1572872 | tf_op jit(solution)/shard_map/ppermute | solution.py:43
  129.1 13.6 %collective-permute-start.28 = (bf16[58,8,256]{2,1,0:T(8,128)(2,1)}, bf16[58,8,256]{2,1,0:T(8,128)(2,1)S(1)}, u32[]{:S(2)}, u32[]{:S(2)}) collective-permute-start(bf16[58,8,256]{2,1,0:T(8,128)(2,1)} %get-tuple-element.26), channel_id=1, source_target_pairs={{0,1},{1,2},{2,3},{3,0},{4,5},{5,6},{6,7},{7,4},{8,9},{9,10},{10,1... | collective-permute-start | bytes 712712 | tf_op jit(solution)/shard_map/ppermute | solution.py:39
  129.5 13.2 %collective-permute-start.29 = (bf16[58,8,256]{2,1,0:T(8,128)(2,1)}, bf16[58,8,256]{2,1,0:T(8,128)(2,1)S(1)}, u32[]{:S(2)}, u32[]{:S(2)}) collective-permute-start(bf16[58,8,256]{2,1,0:T(8,128)(2,1)} %get-tuple-element.27), channel_id=1, source_target_pairs={{0,2},{1,3},{2,0},{3,1},{4,6},{5,7},{6,4},{7,5},{8,10},{9,11},{10,... | collective-permute-start | bytes 712712 | tf_op jit(solution)/shard_map/ppermute | solution.py:39
  130.9 12.2 %collective-permute-start.30 = (bf16[58,8,256]{2,1,0:T(8,128)(2,1)}, bf16[58,8,256]{2,1,0:T(8,128)(2,1)S(1)}, u32[]{:S(2)}, u32[]{:S(2)}) collective-permute-start(bf16[58,8,256]{2,1,0:T(8,128)(2,1)} %get-tuple-element.28), channel_id=1, source_target_pairs={{0,3},{1,0},{2,1},{3,2},{4,7},{5,4},{6,5},{7,6},{8,11},{9,8},{10,9... | collective-permute-start | bytes 712712 | tf_op jit(solution)/shard_map/ppermute | solution.py:39
  143.1 0.9 copy-start.8
  161.8 16.0 %all-to-all-start.3 = ((f32[16,1,512]{2,1,0:T(1,128)}), f32[16,1,512]{2,1,0:T(1,128)S(1)}, u32[]{:S(2)}, u32[]{:S(2)}) async-start(f32[16,1,512]{2,1,0:T(1,128)} %broadcast_in_dim.34), calls=%async_computation.3 | async-start | bytes 65536 | tf_op jit(solution)/shard_map/all_to_all | solution.py:356
  (12 other events, 9.9 us)
